TPU v7x, 128 devices: a whole 4x4x4 slice. The times are simulated.
128 devices in a mesh: tp: 128 (over z, y, x, core).
Axes of the slice: x: 4, y: 4, z: 4, core: 2. Of those that a mesh axis runs over, the one named last changes fastest.
Arguments:
- hidden_in: bfloat16 [1, 1024, 2048], P(None, 'tp')
- lengths: int32 [1], replicated
- attn_norm: bfloat16 [2, 2048], replicated
- w_query: bfloat16 [2, 2048, 32, 64], replicated
- w_key: bfloat16 [2, 2048, 32, 64], replicated
- w_value: bfloat16 [2, 2048, 32, 64], replicated
- w_out: bfloat16 [2, 32, 64, 2048], replicated
- mlp_norm: bfloat16 [2, 2048], replicated
- w_gate: bfloat16 [2, 2048, 8192], P(None, None, 'tp')
- w_up: bfloat16 [2, 2048, 8192], P(None, None, 'tp')
- w_down: bfloat16 [2, 8192, 2048], P(None, 'tp')
- final_norm: bfloat16 [2048], replicated
Outputs:
- output: bfloat16 [1, 1024, 2048], P(None, 'tp')
All inputs are finite; a program needn't handle non-finite values.
Results may differ from a plain program's by a relative error of at most 0.0195171.
Values are sent between devices in bfloat16 or wider.
A program may use at most 1 GiB of HBM per device.

v0:
```python
import jax
import jax.numpy as jnp
from jax import lax
from jax.sharding import PartitionSpec as P

NORM_EPS = 1e-5
ROPE_BASE = 500000.0


def rms_norm(hidden, gain):
    h_wide = hidden.astype(jnp.float32)
    inv_rms = lax.rsqrt(jnp.mean(h_wide * h_wide, axis=-1, keepdims=True) + NORM_EPS)
    return (h_wide * inv_rms * gain.astype(jnp.float32)).astype(jnp.bfloat16)


def rope_tables(positions, head_dim):
    half_dim = head_dim // 2
    inv_freq = ROPE_BASE ** (-2.0 * jnp.arange(half_dim).astype(jnp.float32) / head_dim)
    angles = positions.astype(jnp.float32)[:, None, None] * inv_freq[None, None, :]
    return jnp.cos(angles), jnp.sin(angles)


def rotate(proj, cos_tab, sin_tab):
    half_dim = proj.shape[-1] // 2
    first = proj[..., :half_dim]
    second = proj[..., half_dim:]
    return jnp.concatenate([first * cos_tab - second * sin_tab, second * cos_tab + first * sin_tab], axis=-1)


def attend(q_rot, k_all, v_all, q_pos, lengths):
    head_dim = q_rot.shape[-1]
    key_pos = jnp.arange(k_all.shape[1])
    allowed = (key_pos[None, None, :] <= q_pos[None, :, None]) & (key_pos[None, None, :] < lengths[:, None, None])
    scores = jnp.einsum('bqkgd,bskd->bkgqs', q_rot, k_all, preferred_element_type=jnp.float32) * (head_dim ** -0.5)
    scores = jnp.where(allowed[:, None, None, :, :], scores, -1e30)
    prob_mat = jax.nn.softmax(scores, axis=-1).astype(jnp.bfloat16)
    context = jnp.einsum('bkgqs,bskd->bqkgd', prob_mat, v_all, preferred_element_type=jnp.float32)
    return context.astype(jnp.bfloat16)


def solution(mesh):
    tp_size = mesh.shape['tp']

    def device_fn(hidden_in, lengths, attn_norm, w_query, w_key, w_value, w_out, mlp_norm, w_gate, w_up, w_down, final_norm):
        batch, seq_dev, d_model = hidden_in.shape
        heads = w_query.shape[2]
        head_dim = w_query.shape[3]
        kv_heads = w_key.shape[2]
        groups = heads // kv_heads
        q_pos = lax.axis_index('tp') * seq_dev + jnp.arange(seq_dev)
        cos_tab, sin_tab = rope_tables(q_pos, head_dim)
        hidden = hidden_in
        for layer in range(w_query.shape[0]):
            normed = rms_norm(hidden, attn_norm[layer])
            q_proj = jnp.einsum('bsd,dhe->bshe', normed, w_query[layer], preferred_element_type=jnp.float32)
            k_proj = jnp.einsum('bsd,dhe->bshe', normed, w_key[layer], preferred_element_type=jnp.float32)
            v_proj = jnp.einsum('bsd,dhe->bshe', normed, w_value[layer], preferred_element_type=jnp.float32).astype(jnp.bfloat16)
            q_rot = rotate(q_proj, cos_tab, sin_tab).astype(jnp.bfloat16).reshape(batch, seq_dev, kv_heads, groups, head_dim)
            k_rot = rotate(k_proj, cos_tab, sin_tab).astype(jnp.bfloat16)
            k_all = lax.all_gather(k_rot, 'tp', axis=1, tiled=True)
            v_all = lax.all_gather(v_proj, 'tp', axis=1, tiled=True)
            context = attend(q_rot, k_all, v_all, q_pos, lengths).reshape(batch, seq_dev, heads, head_dim)
            attn_out = jnp.einsum('bshe,hed->bsd', context, w_out[layer], preferred_element_type=jnp.float32)
            hidden = (hidden.astype(jnp.float32) + attn_out).astype(jnp.bfloat16)
            normed = rms_norm(hidden, mlp_norm[layer])
            full_normed = lax.all_gather(normed, 'tp', axis=1, tiled=True)
            gate_proj = jnp.einsum('bsd,df->bsf', full_normed, w_gate[layer], preferred_element_type=jnp.float32)
            up_proj = jnp.einsum('bsd,df->bsf', full_normed, w_up[layer], preferred_element_type=jnp.float32)
            gated_act = (jax.nn.silu(gate_proj) * up_proj).astype(jnp.bfloat16)
            part_out = jnp.einsum('bsf,fd->bsd', gated_act, w_down[layer], preferred_element_type=jnp.float32).astype(jnp.bfloat16)
            part_out = part_out.reshape(batch, tp_size, seq_dev, d_model)
            received = lax.all_to_all(part_out, 'tp', 1, 1, tiled=True)
            mlp_out = jnp.sum(received, axis=1, dtype=jnp.float32)
            hidden = (hidden.astype(jnp.float32) + mlp_out).astype(jnp.bfloat16)
        return rms_norm(hidden, final_norm)

    seq_part = P(None, 'tp', None)
    in_specs = (seq_part, P(), P(), P(), P(), P(), P(), P(), P(None, None, 'tp'), P(None, None, 'tp'), P(None, 'tp', None), P())
    return jax.shard_map(device_fn, mesh=mesh, in_specs=in_specs, out_specs=seq_part, check_vma=False)
```

profile of v0, /device:TPU:1, one launch (start us, length us, event | category | flops | bytes accessed | tf_op | source)
XLA Modules:
  0.0 668.2 jit_solution(16722754384227967018)
XLA Ops:
  6.5 0.0 copy-start
  6.5 0.0 all-gather.9.cloned.1.call-start
  6.5 0.8 slice_convert_fusion.1
  7.3 0.9 fusion.155
  8.2 6.8 %fusion.90 = f32[1,8,32,64]{3,1,2,0:T(8,128)S(1)} fusion(bf16[2,2048,32,64]{1,3,2,0:T(8,128)(2,1)} %param.16, bf16[1,8,2048]{2,1,0:T(8,128)(2,1)} %param.12, f32[2048]{0:T(1024)S(1)} %bitcast.239, f32[8]{0:T(128)S(1)} %add_rsqrt_fusion.4), kind=kOutput, calls=%fused_computation.58 | convolution fusion | flops 67174400 | bytes 8495136 | tf_op jit(solution)/shard_map/bsd,dhe->bshe/dot_general | solution.py:56
  15.0 0.0 copy-done
  15.0 0.0 copy-start.4
  15.0 6.8 %fusion.93 = f32[1,8,32,64]{3,1,2,0:T(8,128)S(1)} fusion(bf16[2,2048,32,64]{1,3,2,0:T(8,128)(2,1)} %param.15, bf16[1,8,2048]{2,1,0:T(8,128)(2,1)S(1)} %copy-done, f32[2048]{0:T(1024)S(1)} %bitcast.240, f32[8]{0:T(128)S(1)} %add_rsqrt_fusion.4), kind=kOutput, calls=%fused_computation.59 | convolution fusion | flops 67174400 | bytes 8495136 | tf_op jit(solution)/shard_map/bsd,dhe->bshe/dot_general | solution.py:55
  21.8 0.1 multiply_cosine_fusion
  21.9 0.1 fusion.161
  22.1 0.7 pad_maximum_fusion
  22.8 0.0 all-gather.9.cloned.1.call-update
  22.8 0.0 all-gather.17.cloned.1.call-start
  22.9 7.4 %fusion.102 = bf16[8,32,64]{2,0,1:T(8,128)(2,1)} fusion(bf16[2,2048,32,64]{1,3,2,0:T(8,128)(2,1)} %param.17, bf16[1,8,2048]{2,1,0:T(8,128)(2,1)S(1)} %copy-done, f32[2048]{0:T(1024)S(1)} %bitcast.241, f32[8]{0:T(128)S(1)} %add_rsqrt_fusion.4), kind=kOutput, calls=%fused_computation.62 | convolution fusion | flops 67190784 | bytes 8462368 | tf_op jit(solution)/shard_map/bsd,dhe->bshe/dot_general | solution.py:57
  30.3 0.0 all-gather.17.cloned.1.call-update
  30.3 0.0 all-gather.11.cloned.1.call-start
  31.0 0.1 fusion.175
  31.1 0.0 copy-done.4
  31.1 73.2 %all-gather.9.cloned.1.call-done = bf16[1,1024,32,64]{3,1,2,0:T(8,128)(2,1)} async-done(((bf16[1,8,32,64]{3,1,2,0:T(8,128)(2,1)}), bf16[1,1024,32,64]{3,1,2,0:T(8,128)(2,1)}) %all-gather.9.cloned.1.call-update) | async-done | bytes 4194320 | tf_op jit(solution)/shard_map/all_gather | solution.py:60
  104.4 5.8 fusion.189
  110.1 0.3 fusion.110
  110.4 0.0 copy-start.1
  110.4 0.0 copy-start.2
  110.5 0.0 copy-start.3
  110.5 74.1 %all-gather.17.cloned.1.call-done = bf16[1024,32,64]{2,0,1:T(8,128)(2,1)} async-done(((bf16[8,32,64]{2,0,1:T(8,128)(2,1)}), bf16[1024,32,64]{2,0,1:T(8,128)(2,1)}) %all-gather.17.cloned.1.call-update) | async-done | bytes 4194320 | tf_op jit(solution)/shard_map/all_gather | solution.py:61
  184.6 7.3 %multiply_reduce_fusion.1 = (f32[8]{0:T(128)S(1)}, f32[1,8,2048]{2,1,0:T(8,128)S(1)}) fusion(bf16[2,32,64,2048]{3,2,1,0:T(8,128)(2,1)} %param.18, bf16[1024,32,64]{2,0,1:T(8,128)(2,1)} %all-gather.17.cloned.1.call-done, f32[1,32,1,8,1024]{4,3,1,2,0:T(8,128)S(1)} %get-tuple-element.28, f32[32,8]{1,0:T(8,128)S(1)} %fusion.110, ...), kind=kOutput, calls=%fused_computation.144 | convolution fusion | flops 101564408 | bytes 17926176 | tf_op jit(solution)/shard_map/bshe,hed->bsd/dot_general | solution.py:63
  191.9 0.7 multiply_convert_fusion.1
  192.6 0.0 all-gather.11.cloned.1.call-update
  192.6 0.2 all-gather.13.cloned.1.call-start
  192.8 66.2 %all-gather.11.cloned.1.call-done = bf16[1,1024,2048]{2,1,0:T(8,128)(2,1)} async-done(((bf16[1,8,2048]{2,1,0:T(8,128)(2,1)}), bf16[1,1024,2048]{2,1,0:T(8,128)(2,1)}) %all-gather.11.cloned.1.call-update) | async-done | bytes 4194320 | tf_op jit(solution)/shard_map/all_gather | solution.py:66
  259.0 0.0 copy-done.1
  259.0 3.6 fusion.34
  262.6 0.0 copy-done.2
  262.6 0.0 copy-done.3
  262.6 6.7 %convert_bitcast_fusion.1 = bf16[1,128,8,2048]{3,2,0,1:T(8,128)(2,1)} fusion(bf16[1,1024,2048]{2,1,0:T(8,128)(2,1)} %all-gather.11.cloned.1.call-done, bf16[2,64,2048]{2,1,0:T(8,128)(2,1)S(1)} %copy-done.2, bf16[2,2048,64]{1,2,0:T(8,128)(2,1)S(1)} %copy-done.3, f32[1024,64]{0,1:T(8,128)S(1)} %fusion.34), kind=kOutput, calls=%fused_computation.39 | convolution fusion | flops 539361280 | bytes 9175040 | tf_op jit(solution)/shard_map/bsf,fd->bsd/dot_general | solution.py:70
  269.4 64.5 %all_to_all.10 = bf16[1,128,8,2048]{3,2,0,1:T(8,128)(2,1)S(1)} all-to-all(bf16[1,128,8,2048]{3,2,0,1:T(8,128)(2,1)} %convert_bitcast_fusion.1), channel_id=1, replica_groups=mesh['tp'=128] {'tp'}, dimensions={1} | all-to-all | bytes 8388608 | tf_op jit(solution)/shard_map/all_to_all | solution.py:72
  333.8 0.6 convert_reduce_fusion.1
  334.5 0.1 fusion.158
  334.6 6.7 %fusion.96 = f32[1,8,32,64]{3,1,2,0:T(8,128)S(1)} fusion(bf16[2,2048,32,64]{1,3,2,0:T(8,128)(2,1)} %param.16, bf16[1,8,2048]{2,1,0:T(8,128)(2,1)S(1)} %get-tuple-element.8, f32[2048]{0:T(1024)S(1)} %bitcast.236, f32[8]{0:T(128)S(1)} %add_rsqrt_fusion.2), kind=kOutput, calls=%fused_computation.60 | convolution fusion | flops 67174400 | bytes 8495136 | tf_op jit(solution)/shard_map/bsd,dhe->bshe/dot_general | solution.py:56
  341.4 6.8 %fusion.99 = f32[1,8,32,64]{3,1,2,0:T(8,128)S(1)} fusion(bf16[2,2048,32,64]{1,3,2,0:T(8,128)(2,1)} %param.15, bf16[1,8,2048]{2,1,0:T(8,128)(2,1)S(1)} %get-tuple-element.8, f32[2048]{0:T(1024)S(1)} %bitcast.237, f32[8]{0:T(128)S(1)} %add_rsqrt_fusion.2), kind=kOutput, calls=%fused_computation.61 | convolution fusion | flops 67174400 | bytes 8495136 | tf_op jit(solution)/shard_map/bsd,dhe->bshe/dot_general | solution.py:55
  348.1 0.2 fusion.163
  348.3 0.7 pad_maximum_fusion.1
  349.0 0.0 all-gather.13.cloned.1.call-update
  349.0 0.0 all-gather.19.cloned.1.call-start
  349.1 7.4 %fusion.105 = bf16[8,32,64]{2,0,1:T(8,128)(2,1)} fusion(bf16[2,2048,32,64]{1,3,2,0:T(8,128)(2,1)} %param.17, bf16[1,8,2048]{2,1,0:T(8,128)(2,1)S(1)} %get-tuple-element.8, f32[2048]{0:T(1024)S(1)} %bitcast.238, f32[8]{0:T(128)S(1)} %add_rsqrt_fusion.2), kind=kOutput, calls=%fused_computation.63 | convolution fusion | flops 67190784 | bytes 8462368 | tf_op jit(solution)/shard_map/bsd,dhe->bshe/dot_general | solution.py:57
  356.5 0.0 all-gather.19.cloned.1.call-update
  356.5 0.3 all-gather.15.cloned.1.call-start
  356.8 71.8 %all-gather.13.cloned.1.call-done = bf16[1,1024,32,64]{3,1,2,0:T(8,128)(2,1)} async-done(((bf16[1,8,32,64]{3,1,2,0:T(8,128)(2,1)}), bf16[1,1024,32,64]{3,1,2,0:T(8,128)(2,1)}) %all-gather.13.cloned.1.call-update) | async-done | bytes 4194320 | tf_op jit(solution)/shard_map/all_gather | solution.py:60
  428.5 5.8 fusion.192
  434.3 0.3 fusion.111
  434.6 74.0 %all-gather.19.cloned.1.call-done = bf16[1024,32,64]{2,0,1:T(8,128)(2,1)} async-done(((bf16[8,32,64]{2,0,1:T(8,128)(2,1)}), bf16[1024,32,64]{2,0,1:T(8,128)(2,1)}) %all-gather.19.cloned.1.call-update) | async-done | bytes 4194320 | tf_op jit(solution)/shard_map/all_gather | solution.py:61
  508.6 7.3 %multiply_reduce_fusion = (f32[8]{0:T(128)S(1)}, f32[1,8,2048]{2,1,0:T(8,128)S(1)}) fusion(bf16[2,32,64,2048]{3,2,1,0:T(8,128)(2,1)} %param.18, bf16[1024,32,64]{2,0,1:T(8,128)(2,1)} %all-gather.19.cloned.1.call-done, f32[1,32,1,8,1024]{4,3,1,2,0:T(8,128)S(1)} %get-tuple-element.32, f32[32,8]{1,0:T(8,128)S(1)} %fusion.111, ...), kind=kOutput, calls=%fused_computation.142 | convolution fusion | flops 101564408 | bytes 17926176 | tf_op jit(solution)/shard_map/bshe,hed->bsd/dot_general | solution.py:63
  515.9 0.7 multiply_convert_fusion
  516.6 0.0 all-gather.15.cloned.1.call-update
  516.6 66.4 %all-gather.15.cloned.1.call-done = bf16[1,1024,2048]{2,1,0:T(8,128)(2,1)} async-done(((bf16[1,8,2048]{2,1,0:T(8,128)(2,1)}), bf16[1,1024,2048]{2,1,0:T(8,128)(2,1)}) %all-gather.15.cloned.1.call-update) | async-done | bytes 4194320 | tf_op jit(solution)/shard_map/all_gather | solution.py:66
  583.1 3.6 fusion.30
  586.6 0.0 copy-start.5
  586.7 6.7 %convert_bitcast_fusion = bf16[1,128,8,2048]{3,2,0,1:T(8,128)(2,1)} fusion(bf16[1,1024,2048]{2,1,0:T(8,128)(2,1)} %all-gather.15.cloned.1.call-done, bf16[2,64,2048]{2,1,0:T(8,128)(2,1)S(1)} %copy-done.2, bf16[2,2048,64]{1,2,0:T(8,128)(2,1)S(1)} %copy-done.3, f32[1024,64]{0,1:T(8,128)S(1)} %fusion.30), kind=kOutput, calls=%fused_computation.38 | convolution fusion | flops 539361280 | bytes 9175040 | tf_op jit(solution)/shard_map/bsf,fd->bsd/dot_general | solution.py:70
  593.3 5.8 all-to-all-start.1
  599.1 0.0 copy-done.5
  599.1 58.6 %all-to-all-done.1 = bf16[1,128,8,2048]{3,2,0,1:T(8,128)(2,1)} async-done(((bf16[1,128,8,2048]{3,2,0,1:T(8,128)(2,1)}), bf16[1,128,8,2048]{3,2,0,1:T(8,128)(2,1)}, u32[]{:S(2)}, u32[]{:S(2)}) %all-to-all-start.1) | async-done | bytes 4194336 | tf_op jit(solution)/shard_map/all_to_all | solution.py:72
  657.7 2.8 convert_reduce_fusion
  660.6 0.1 fusion.152
  660.7 0.7 fusion.154
  (11 shorter events, 0.1 us)
Async XLA Ops:
  6.5 8.5 %copy-start = (bf16[1,8,2048]{2,1,0:T(8,128)(2,1)S(1)}, bf16[1,8,2048]{2,1,0:T(8,128)(2,1)}, u32[]{:S(2)}) copy-start(bf16[1,8,2048]{2,1,0:T(8,128)(2,1)} %param.12) | copy-start | bytes 98308
  6.5 97.8 %all-gather.9.cloned.1.call-start = ((), (), s32[]{:S(2)}) async-start(), calls=%async_computation.2 | async-start | bytes 8454144 | tf_op jit(solution)/shard_map/all_gather | solution.py:60
  15.0 16.1 %copy-start.4 = (bf16[2,2048]{1,0:T(2,128)(2,1)S(1)}, bf16[2,2048]{1,0:T(2,128)(2,1)}, u32[]{:S(2)}) copy-start(bf16[2,2048]{1,0:T(2,128)(2,1)} %param.19) | copy-start | bytes 24580
  22.8 161.7 %all-gather.17.cloned.1.call-start = ((), (), s32[]{:S(2)}) async-start(), calls=%async_computation.6 | async-start | bytes 8454144 | tf_op jit(solution)/shard_map/all_gather | solution.py:61
  30.3 228.8 %all-gather.11.cloned.1.call-start = ((), (), s32[]{:S(2)}) async-start(), calls=%async_computation.3 | async-start | bytes 4227072 | tf_op jit(solution)/shard_map/all_gather | solution.py:66
  110.4 148.6 %copy-start.1 = (bf16[2,2048,64]{1,2,0:T(8,128)(2,1)S(1)}, bf16[2,2048,64]{1,2,0:T(8,128)(2,1)}, u32[]{:S(2)}) copy-start(bf16[2,2048,64]{1,2,0:T(8,128)(2,1)} %param.20) | copy-start | bytes 1572868
  110.4 152.2 %copy-start.2 = (bf16[2,64,2048]{2,1,0:T(8,128)(2,1)S(1)}, bf16[2,64,2048]{2,1,0:T(8,128)(2,1)}, u32[]{:S(2)}) copy-start(bf16[2,64,2048]{2,1,0:T(8,128)(2,1)} %param.22) | copy-start | bytes 1572868
  110.5 152.2 %copy-start.3 = (bf16[2,2048,64]{1,2,0:T(8,128)(2,1)S(1)}, bf16[2,2048,64]{1,2,0:T(8,128)(2,1)}, u32[]{:S(2)}) copy-start(bf16[2,2048,64]{1,2,0:T(8,128)(2,1)} %param.21) | copy-start | bytes 1572868
  192.6 235.9 %all-gather.13.cloned.1.call-start = ((), (), s32[]{:S(2)}) async-start(), calls=%async_computation.4 | async-start | bytes 8454144 | tf_op jit(solution)/shard_map/all_gather | solution.py:60
  349.0 159.6 %all-gather.19.cloned.1.call-start = ((), (), s32[]{:S(2)}) async-start(), calls=%async_computation.7 | async-start | bytes 8454144 | tf_op jit(solution)/shard_map/all_gather | solution.py:61
  356.5 226.6 %all-gather.15.cloned.1.call-start = ((), (), s32[]{:S(2)}) async-start(), calls=%async_computation.5 | async-start | bytes 4227072 | tf_op jit(solution)/shard_map/all_gather | solution.py:66
  586.6 12.5 %copy-start.5 = (bf16[2048]{0:T(1024)(128)(2,1)S(1)}, bf16[2048]{0:T(1024)(128)(2,1)}, u32[]{:S(2)}) copy-start(bf16[2048]{0:T(1024)(128)(2,1)} %param.23) | copy-start | bytes 12292
  593.3 64.4 %all-to-all-start.1 = ((bf16[1,128,8,2048]{3,2,0,1:T(8,128)(2,1)}), bf16[1,128,8,2048]{3,2,0,1:T(8,128)(2,1)}, u32[]{:S(2)}, u32[]{:S(2)}) async-start(bf16[1,128,8,2048]{3,2,0,1:T(8,128)(2,1)} %convert_bitcast_fusion), calls=%async_computation.1 | async-start | bytes 8388608 | tf_op jit(solution)/shard_map/all_to_all | solution.py:72
Sparse Core Ops, SparseCore 0:
  22.9 81.3 all-gather.8
  107.2 77.3 all-gather.16
  192.7 66.2 all-gather.10
  349.1 79.3 all-gather.12
  431.2 77.3 all-gather.18
  516.7 66.2 all-gather.14
where the time goes:
time: 670 us; the launch traced here: 668 us
  waiting for transfers between devices  484 us (72%)
  matrix products  88.5 us (13%)
  blocking collectives  64.5 us (10%)
  between operations  14.3 us (2%)
  other arithmetic  10.2 us (2%)
    all_gather x2, waiting for transfers between devices, device_fn(): v_all = lax.all_gather(v_proj, 'tp', axis=1, tiled=True)  148 us
    all_gather x2, waiting for transfers between devices, device_fn(): k_all = lax.all_gather(k_rot, 'tp', axis=1, tiled=True)  145 us
    all_gather x2, waiting for transfers between devices, device_fn(): full_normed = lax.all_gather(normed, 'tp', axis=1, tiled=True)  133 us
    all_to_all x1, blocking collectives, device_fn(): received = lax.all_to_all(part_out, 'tp', 1, 1, tiled=True)  64.5 us
    all_to_all x1, waiting for transfers between devices, device_fn(): received = lax.all_to_all(part_out, 'tp', 1, 1, tiled=True)  58.6 us
    dot_general x2, matrix products, device_fn(): jnp.einsum('bsd,dhe->bshe', normed, w_value[layer], preferred_element_typ...  14.8 us
    dot_general x2, matrix products, device_fn(): jnp.einsum('bshe,hed->bsd', context, w_out[layer], preferred_element_type...  14.6 us
    dot_general x2, matrix products, device_fn(): jnp.einsum('bsd,dhe->bshe', normed, w_query[layer], preferred_element_typ...  13.5 us
  transfers between devices with their start and end apart: 7, of which 7 were waited for; matrix products, arithmetic and copies ran while one was open for 4% of the time, Pallas kernels for 0%

commit v1 on v0

v1 whole, which is shorter than its diff:
```python
import functools

import jax
import jax.numpy as jnp
import numpy as np
from jax import lax
from jax.experimental import pallas as pl
from jax.experimental.pallas import tpu as pltpu
from jax.sharding import PartitionSpec as P

NORM_EPS = 1e-5
ROPE_BASE = 500000.0
MESH = pl.DeviceIdType.MESH
NX, NY, NZ = 4, 4, 4
ROW = 2 * NX
COL = NY * NZ

ROW_STEPS = [(2, 1), (2, 0), (1, 1), (3, 1), (1, 0), (3, 0), (0, 1)]
COL_STEPS = sorted(((dz, dy) for dz in range(NZ) for dy in range(NY) if dz or dy),
                   key=lambda s: -(min(s[0], 4 - s[0]) + min(s[1], 4 - s[1])))


def bf(v):
    return v.astype(jnp.bfloat16)


def f32(v):
    return v.astype(jnp.float32)


def dot_nt(a, b):
    return lax.dot_general(a, b, (((1,), (1,)), ((), ())), preferred_element_type=jnp.float32)


def norm_rows(h, gain):
    inv = lax.rsqrt(jnp.mean(h * h, axis=-1, keepdims=True) + NORM_EPS)
    return h * inv * gain


def kernel(h_ref, len_ref, gattn_ref, gmlp_ref, gfin_ref, freq_ref, wq_ref, wk_ref, wv_ref, wo_ref, wg_ref, wu_ref, wd_ref,
           out_ref,
           hrow, wq_s, wk_s, wv_s, wo_s, wm, kbuf, vbuf, cs, cbuf, hloc, hcol, zs, ps, acts, ysend, ybuf,
           lsem, wosem, msem, asend, arecv, ksend, krecv, vsend, vrecv, csend, crecv, hsend, hrecv, ssend, srecv, gsend, grecv):
    layers = wo_s.shape[0]
    tok, d_model = h_ref.shape
    rtok = ROW * tok
    units = wm.shape[3]
    me = lax.axis_index('tp')
    core = lax.rem(me, 2)
    i = lax.rem(me, ROW)
    x = i // 2
    r = me // ROW
    y = lax.rem(r, NY)
    z = r // NY

    def row_id(dx, dc):
        return 2 * lax.rem(x + dx, NX) + (1 - core if dc else core)

    def row_dev(dx, dc):
        return (r * ROW + row_id(dx, dc),)

    def col_row(dz, dy):
        return NY * lax.rem(z + dz, NZ) + lax.rem(y + dy, NY)

    def col_dev(dz, dy):
        return (col_row(dz, dy) * ROW + i,)

    def send(src, dst, ssem, rsem, dev):
        pltpu.make_async_remote_copy(src_ref=src, dst_ref=dst, send_sem=ssem, recv_sem=rsem, device_id=dev,
                                     device_id_type=MESH).start()

    def wait(ref, sem):
        pltpu.make_async_copy(ref, ref, sem).wait()

    heads = 4
    half = 32
    local = []

    def load(src, dst, sem):
        c = pltpu.make_async_copy(src, dst, sem)
        c.start()
        return c

    def load_qkv(l):
        base = i * (2 * heads * half)
        got = []
        for k, (src, dst) in enumerate(((wq_ref, wq_s), (wk_ref, wk_s))):
            for j in range(heads):
                for s in range(2):
                    got.append(load(src.at[l, pl.ds(base + (2 * j + s) * half, half)],
                                    dst.at[l, pl.ds((s * heads + j) * half, half)], lsem.at[l, 9 * k + 2 * j + s]))
        got.append(load(wv_ref.at[l, pl.ds(base, 2 * heads * half)], wv_s.at[l], lsem.at[l, 8]))
        return got

    def load_mlp(l):
        return [load(w.at[l], wm.at[l, i, k], msem.at[l, k]) for k, w in enumerate((wg_ref, wu_ref, wd_ref))]

    qkv_loads = [load_qkv(0)]
    mlp_loads = [load_mlp(0), load_mlp(1)]
    wo_loads = [load(wo_ref.at[0], wo_s.at[0], wosem.at[0])]
    qkv_loads.append(load_qkv(1))
    wo_loads.append(load(wo_ref.at[1], wo_s.at[1], wosem.at[1]))

    kbuf[...] = jnp.zeros_like(kbuf)
    vbuf[...] = jnp.zeros_like(vbuf)
    barrier = pltpu.get_barrier_semaphore()
    for s in ROW_STEPS:
        pl.semaphore_signal(barrier, inc=1, device_id=row_dev(*s), device_id_type=MESH)
    for s in COL_STEPS:
        pl.semaphore_signal(barrier, inc=1, device_id=col_dev(*s), device_id_type=MESH)
    hrow[pl.ds(i, 1)] = h_ref[...][None]
    pos = f32(r * rtok + lax.broadcasted_iota(jnp.int32, (rtok, 1), 0))
    angles = pos * freq_ref[...]
    cos_tab = jnp.cos(angles)
    sin_tab = jnp.sin(angles)
    pl.semaphore_wait(barrier, len(ROW_STEPS) + len(COL_STEPS))

    def slot(dx, dc):
        return row_id((dx + NX) % NX, dc)

    hu = units // 2

    def g_send(l):
        for c in mlp_loads[l]:
            c.wait()
        own = wm.at[l, i]
        send(own, own, gsend.at[l, 1], grecv.at[l, 1], row_dev(1, 0))
        send(own, own, gsend.at[l, 2], grecv.at[l, 2], row_dev(3, 0))
        send(own, own, gsend.at[l, 0], grecv.at[l, 0], row_dev(0, 1))

    def g_fwd(l):
        a = wm.at[l, slot(-1, 0)]
        ah = wm.at[l, slot(-1, 0), :, pl.ds(0, hu)]
        b = wm.at[l, slot(1, 0)]
        bh = wm.at[l, slot(1, 0), :, pl.ds(hu, hu)]
        wait(a, grecv.at[l, 1])
        send(ah, ah, gsend.at[l, 3], grecv.at[l, 3], row_dev(1, 0))
        wait(b, grecv.at[l, 2])
        send(bh, bh, gsend.at[l, 4], grecv.at[l, 4], row_dev(3, 0))
        send(a, a, gsend.at[l, 5], grecv.at[l, 5], row_dev(0, 1))
        send(b, b, gsend.at[l, 6], grecv.at[l, 6], row_dev(0, 1))

    def g_halves(l, dc):
        s = slot(2, dc)
        return wm.at[l, s, :, pl.ds(0, hu)], wm.at[l, s, :, pl.ds(hu, hu)]

    def g_fwd2(l):
        for k, ref in enumerate(g_halves(l, 0)):
            wait(ref, grecv.at[l, 3 + k])
            send(ref, ref, gsend.at[l, 7 + k], grecv.at[l, 7 + k], row_dev(0, 1))

    def g_done(l):
        wait(wm.at[l, slot(0, 1)], grecv.at[l, 0])
        wait(wm.at[l, slot(-1, 1)], grecv.at[l, 5])
        wait(wm.at[l, slot(1, 1)], grecv.at[l, 6])
        for k, ref in enumerate(g_halves(l, 1)):
            wait(ref, grecv.at[l, 7 + k])
        for k in (0, 1, 2, 5, 6):
            wait(wm.at[l, i], gsend.at[l, k])
        for k in (3, 4, 7, 8):
            wait(wm.at[l, i, :, pl.ds(0, hu)], gsend.at[l, k])

    lane = lax.broadcasted_iota(jnp.int32, (1, 2 * heads * half), 1)
    length = len_ref[0]

    hidden = f32(h_ref[...])
    for l in range(layers):
        g_attn = f32(gattn_ref[...])[l:l + 1]
        g_mlp = f32(gmlp_ref[...])[l:l + 1]
        own = h_ref if l == 0 else hloc.at[0]
        for k, s in enumerate(ROW_STEPS):
            send(own, hrow.at[i], asend.at[k], arecv.at[k], row_dev(*s))
        for k, (dx, dc) in enumerate(ROW_STEPS):
            wait(hrow.at[slot(-dx, dc)], arecv.at[k])
        if l == 0:
            g_send(0)
        else:
            g_fwd(1)
        zrow = bf(norm_rows(f32(hrow[...]).reshape(rtok, d_model), g_attn))
        zs[0:rtok] = zrow
        for c in qkv_loads[l]:
            c.wait()

        def rotated(w):
            p = dot_nt(zs[0:rtok], w)
            a, b = p[:, :heads * half], p[:, heads * half:]
            return bf(jnp.concatenate([a * cos_tab - b * sin_tab, b * cos_tab + a * sin_tab], axis=1))

        kbuf[pl.ds(r, 1)] = rotated(wk_s[l])[None]
        vbuf[pl.ds(r, 1)] = bf(dot_nt(zs[0:rtok], wv_s[l]))[None]
        for k, (dz, dy) in enumerate(COL_STEPS):
            to = col_row(dz, dy)

            @pl.when(to > r)
            def _():
                send(kbuf.at[r], kbuf.at[r], ksend.at[k], krecv.at[k], col_dev(dz, dy))
                send(vbuf.at[r], vbuf.at[r], vsend.at[k], vrecv.at[k], col_dev(dz, dy))

        q_rot = rotated(wq_s[l])
        q_all = jnp.concatenate(
            [jnp.where(lax.rem(lane, heads * half) // half == j, q_rot, jnp.zeros_like(q_rot)) for j in range(heads)], axis=0)
        for k, (dz, dy) in enumerate(COL_STEPS):
            frm = col_row(NZ - dz, NY - dy)

            @pl.when(frm < r)
            def _():
                wait(kbuf.at[frm], krecv.at[k])
                wait(vbuf.at[frm], vrecv.at[k])

        keys = kbuf.shape[0] * rtok
        scores = dot_nt(q_all, kbuf[...].reshape(keys, 2 * heads * half)) * (2 * half) ** -0.5
        k_pos = lax.broadcasted_iota(jnp.int32, scores.shape, 1)
        q_pos = r * rtok + lax.rem(lax.broadcasted_iota(jnp.int32, scores.shape, 0), rtok)
        scores = jnp.where((k_pos <= q_pos) & (k_pos < length), scores, -1e30)
        e = jnp.exp(scores - jnp.max(scores, axis=-1, keepdims=True))
        probs = bf(e * (1.0 / jnp.sum(e, axis=-1, keepdims=True)))
        pv = jnp.dot(probs, vbuf[...].reshape(keys, 2 * heads * half), preferred_element_type=jnp.float32)
        ctx = jnp.zeros((rtok, 2 * heads * half), jnp.float32)
        for j in range(heads):
            ctx = jnp.where(lane // (2 * half) == j, pv[j * rtok:(j + 1) * rtok], ctx)
        cs[...] = bf(ctx.reshape(ROW, tok, 2 * heads * half))
        for k, s in enumerate(ROW_STEPS):
            send(cs.at[row_id(*s)], cbuf.at[i], csend.at[k], crecv.at[k], row_dev(*s))
        cbuf[pl.ds(i, 1)] = cs[pl.ds(i, 1)]
        wo_loads[l].wait()
        for k, (dx, dc) in enumerate(ROW_STEPS):
            wait(cbuf.at[slot(-dx, dc)], crecv.at[k])
        if l == 0:
            g_fwd(0)
            g_send(1)
        ctx_all = jnp.concatenate([cbuf[k] for k in range(ROW)], axis=1)
        attn_out = jnp.dot(ctx_all, wo_s[l], preferred_element_type=jnp.float32)
        hid_b = bf(hidden + attn_out)
        hidden = f32(hid_b)
        hloc[1] = hid_b
        hcol[0] = hid_b
        for k, s in enumerate(COL_STEPS):
            send(hloc.at[1], hcol.at[k + 1], hsend.at[k], hrecv.at[k], col_dev(*s))
        g_fwd2(l)
        for k in range(COL - 1):
            wait(hcol.at[k + 1], hrecv.at[k])
        zs[...] = bf(norm_rows(f32(hcol[...]).reshape(COL * tok, d_model), g_mlp))
        g_done(l)
        grp = ROW // 2
        for b in range(2):
            gate = dot_nt(zs[...], wm[l, b * grp:(b + 1) * grp, 0].reshape(grp * units, d_model))
            up = dot_nt(zs[...], wm[l, b * grp:(b + 1) * grp, 1].reshape(grp * units, d_model))
            act = bf(gate * (1.0 / (1.0 + jnp.exp(-gate))) * up)
            for j in range(grp):
                acts[b, j * COL * tok:(j + 1) * COL * tok] = jnp.where(lane // units == j, act, jnp.zeros_like(act))
        parts = 4
        width = d_model // parts
        for n in range(parts):
            cols = slice(n * width, (n + 1) * width)
            total = jnp.zeros((COL * tok, width), jnp.float32)
            for b in range(2):
                wd = wm[l, b * grp:(b + 1) * grp, 2, :, cols].reshape(grp * units, width)
                prod = jnp.dot(acts[b], wd, preferred_element_type=jnp.float32)
                for j in range(grp):
                    total = total + f32(bf(prod[j * COL * tok:(j + 1) * COL * tok]))
            ysend[:, :, cols] = total.reshape(COL, tok, width)
            for k, (dz, dy) in enumerate(COL_STEPS):
                send(ysend.at[k + 1, :, cols], ybuf.at[k, :, cols], ssend.at[k], srecv.at[k], col_dev(NZ - dz, NY - dy))
        total = ysend[0]
        for k in range(COL - 1):
            wait(ybuf.at[k], srecv.at[k])
            total = total + ybuf[k]
        hid_b = bf(hidden + total)
        hidden = f32(hid_b)
        for k in range(ROW - 1):
            wait(own, asend.at[k])
            wait(cs.at[0], csend.at[k])
        for k, (dz, dy) in enumerate(COL_STEPS):
            @pl.when(col_row(dz, dy) > r)
            def _():
                wait(kbuf.at[r], ksend.at[k])
                wait(vbuf.at[r], vsend.at[k])
            wait(hloc.at[1], hsend.at[k])
            wait(ysend.at[0], ssend.at[k])
        if l < layers - 1:
            hloc[0] = hid_b
            hrow[pl.ds(i, 1)] = hid_b[None]
    out_ref[...] = bf(norm_rows(hidden, f32(gfin_ref[...])))


def solution(mesh):
    def device_fn(hidden_in, lengths, attn_norm, w_query, w_key, w_value, w_out, mlp_norm, w_gate, w_up, w_down, final_norm):
        batch, tok, d_model = hidden_in.shape
        layers, _, heads, head_dim = w_query.shape
        units = w_gate.shape[2]
        half = head_dim // 2
        freq = ROPE_BASE ** (-2.0 * np.arange(half, dtype=np.float32) / head_dim)
        freq = jnp.asarray(np.tile(freq.astype(np.float32), heads // ROW)[None])

        def by_rows(w):
            return jnp.transpose(w, (0, 2, 3, 1)).reshape(layers, heads * head_dim, d_model)

        wide = heads * head_dim // ROW
        dma = pltpu.SemaphoreType.DMA
        b16 = jnp.bfloat16
        vm = pl.BlockSpec(memory_space=pltpu.VMEM)
        hbm = pl.BlockSpec(memory_space=pl.ANY)
        rtok = ROW * tok
        out = pl.pallas_call(
            kernel,
            name='prefill',
            out_shape=jax.ShapeDtypeStruct((tok, d_model), b16),
            in_specs=[vm, pl.BlockSpec(memory_space=pltpu.SMEM), vm, vm, vm, vm] + [hbm] * 7,
            out_specs=vm,
            scratch_shapes=[
                pltpu.VMEM((ROW, tok, d_model), b16),
                pltpu.VMEM((layers, wide, d_model), b16),
                pltpu.VMEM((layers, wide, d_model), b16),
                pltpu.VMEM((layers, wide, d_model), b16),
                pltpu.VMEM((layers, heads * head_dim, d_model), b16),
                pltpu.VMEM((layers, ROW, 3, units, d_model), b16),
                pltpu.VMEM((COL, rtok, wide), b16),
                pltpu.VMEM((COL, rtok, wide), b16),
                pltpu.VMEM((ROW, tok, wide), b16),
                pltpu.VMEM((ROW, tok, wide), b16),
                pltpu.VMEM((2, tok, d_model), b16),
                pltpu.VMEM((COL, tok, d_model), b16),
                pltpu.VMEM((COL * tok, d_model), b16),
                pltpu.VMEM((8, 128), b16),
                pltpu.VMEM((2, ROW // 2 * COL * tok, ROW // 2 * units), b16),
                pltpu.VMEM((COL, tok, d_model), jnp.float32),
                pltpu.VMEM((COL - 1, tok, d_model), jnp.float32),
                dma((layers, 18)), dma((layers,)), dma((layers, 3)),
                dma((ROW - 1,)), dma((ROW - 1,)),
                dma((COL - 1,)), dma((COL - 1,)), dma((COL - 1,)), dma((COL - 1,)),
                dma((ROW - 1,)), dma((ROW - 1,)),
                dma((COL - 1,)), dma((COL - 1,)),
                dma((COL - 1,)), dma((COL - 1,)),
                dma((layers, 9)), dma((layers, 9)),
            ],
            compiler_params=pltpu.CompilerParams(collective_id=0, has_side_effects=True, vmem_limit_bytes=60 * 1024 * 1024),
        )(hidden_in.reshape(tok, d_model), lengths, attn_norm, mlp_norm, final_norm.reshape(1, d_model), freq,
          by_rows(w_query), by_rows(w_key), by_rows(w_value), w_out.reshape(layers, heads * head_dim, d_model),
          jnp.transpose(w_gate, (0, 2, 1)), jnp.transpose(w_up, (0, 2, 1)), w_down)
        return out.reshape(batch, tok, d_model)

    seq_part = P(None, 'tp', None)
    in_specs = (seq_part, P(), P(), P(), P(), P(), P(), P(), P(None, None, 'tp'), P(None, None, 'tp'), P(None, 'tp', None), P())
    return jax.shard_map(device_fn, mesh=mesh, in_specs=in_specs, out_specs=seq_part, check_vma=False)
```

time: 670 us -> 121 us (0.18)
  waiting for transfers between devices: 484 us -> 0 us
  Pallas kernels: 0 us -> 117 us
  matrix products: 88.5 us -> 0 us
  blocking collectives: 64.5 us -> 0 us
  between operations: 14.3 us -> 0.66 us
  other arithmetic: 10.2 us -> 0 us
    all_gather x6 -> x0, waiting for transfers between devices: 426 us -> none  [the longest x2 148 us: device_fn(): v_all = lax.all_gather(v_proj, 'tp', axis=1, tiled=True)]
    pallas_call x0 -> x1, Pallas kernels: none -> 117 us  [device_fn(): pl.pallas_call(kernel, name='prefill', out_shape=jax.ShapeDtypeStruct((to...]
    dot_general x14 -> x0, matrix products: 88.5 us -> none  [the longest x2 14.8 us: device_fn(): jnp.einsum('bsd,dhe->bshe', normed, w_value[layer], preferred_element_typ...]
    all_to_all x1 -> x0, blocking collectives: 64.5 us -> none  [device_fn(): received = lax.all_to_all(part_out, 'tp', 1, 1, tiled=True)]
    all_to_all x1 -> x0, waiting for transfers between devices: 58.6 us -> none  [device_fn(): received = lax.all_to_all(part_out, 'tp', 1, 1, tiled=True)]
  transfers between devices with their start and end apart: 7 -> 0, of which waited for: 7 -> 0; matrix products, arithmetic and copies ran while one was open for 4% -> 0% of each run, Pallas kernels for 0% -> 0%
where the time goes in v1:
time: 121 us
  Pallas kernels  117 us (97%)
  local copies, waits for them, and re-layouts  2.67 us (2%)
    pallas_call x1, Pallas kernels, device_fn(): pl.pallas_call(kernel, name='prefill', out_shape=jax.ShapeDtypeStruct((to...  117 us

profile of v1, /device:TPU:1, one launch (start us, length us, event | category | flops | bytes accessed | tf_op | source)
XLA Modules:
  0.0 120.8 jit_solution(4995454622346437550)
XLA Ops:
  0.7 1.3 %reshape.22.gfin_ref = bf16[1,2048]{1,0:T(2,128)(2,1)} reshape(bf16[2048]{0:T(1024)(128)(2,1)} %param.24) | data formatting | bytes 8192 | tf_op jit(solution)/shard_map/reshape | solution.py:337
  1.9 117.5 %prefill.1 = bf16[8,2048]{1,0:T(8,128)(2,1)} custom-call(bf16[8,2048]{1,0:T(8,128)(2,1)} %bitcast.21, s32[1]{0:T(128)S(6)} %copy.15.len_ref, bf16[2,2048]{1,0:T(2,128)(2,1)} %gattn_ref.1, bf16[2,2048]{1,0:T(2,128)(2,1)} %gmlp_ref.1, bf16[1,2048]{1,0:T(2,128)(2,1)} %reshape.22.gfin_ref, f32[1,128]{1,0:T(1,128)} %constant.2.clone.freq_ref, ...), custom_call_target="tpu_custom_call" | custom-call | tf_op jit(solution)/shard_map/prefill/pallas_call | solution.py:304
  119.4 1.4 %copy.16 = bf16[1,8,2048]{2,1,0:T(8,128)(2,1)} copy(bf16[1,8,2048]{2,1,0:T(8,128)(2,1)} %bitcast.20) | data formatting | bytes 65536

commit v2 on v1

v2 whole, which is shorter than its diff:
```python
import functools

import jax
import jax.numpy as jnp
import numpy as np
from jax import lax
from jax.experimental import pallas as pl
from jax.experimental.pallas import tpu as pltpu
from jax.sharding import PartitionSpec as P

NORM_EPS = 1e-5
ROPE_BASE = 500000.0
MESH = pl.DeviceIdType.MESH
NX, NY, NZ = 4, 4, 4
ROW = 2 * NX
COL = NY * NZ

ROW_STEPS = [(2, 1), (2, 0), (1, 1), (3, 1), (1, 0), (3, 0), (0, 1)]
COL_STEPS = sorted(((dz, dy) for dz in range(NZ) for dy in range(NY) if dz or dy),
                   key=lambda s: -(min(s[0], 4 - s[0]) + min(s[1], 4 - s[1])))
PLANE_STEPS = sorted(((dy, dx, dc) for dy in range(NY) for dx in range(NX) for dc in range(2) if dy or dx or dc),
                     key=lambda s: -(min(s[0], 4 - s[0]) + min(s[1], 4 - s[1])))


class Phases:
    def __init__(self):
        self.open = None

    def __call__(self, name=None):
        if self.open is not None:
            self.open.__exit__(None, None, None)
        self.open = jax.named_scope(name) if name else None
        if name:
            self.open.__enter__()


def bf(v):
    return v.astype(jnp.bfloat16)


def f32(v):
    return v.astype(jnp.float32)


def dot_nt(a, b):
    return lax.dot_general(a, b, (((1,), (1,)), ((), ())), preferred_element_type=jnp.float32)


def norm_rows(h, gain):
    inv = lax.rsqrt(jnp.mean(h * h, axis=-1, keepdims=True) + NORM_EPS)
    return h * inv * gain


def kernel(h_ref, len_ref, gattn_ref, gmlp_ref, gfin_ref, freq_ref, wq_ref, wk_ref, wv_ref, wo_ref, wg_ref, wu_ref, wd_ref,
           out_ref,
           hrow, wq_s, wkv_s, wo_s, wm, kvs, kvbuf, qs, qbuf, cs, cbuf, hloc, hcol, zs, acts, ysend, ybuf,
           lsem, wosem, msem, asend, arecv, kvsend, kvrecv, qsend, qrecv, csend, crecv, hsend, hrecv, ssend, srecv, gsend, grecv):
    phase = Phases()
    phase('start')
    layers = wo_s.shape[0]
    tok, d_model = h_ref.shape
    rtok = ROW * tok
    heads, wide = kvs.shape[0], kvs.shape[2]
    hd = wide // 2
    half = hd // 2
    units = wm.shape[3]
    me = lax.axis_index('tp')
    core = lax.rem(me, 2)
    i = lax.rem(me, ROW)
    x = i // 2
    r = me // ROW
    y = lax.rem(r, NY)
    z = r // NY

    def row_id(dx, dc):
        return 2 * lax.rem(x + (dx + NX) % NX, NX) + (1 - core if dc else core)

    def row_dev(dx, dc):
        return (r * ROW + row_id(dx, dc),)

    def y_at(dy):
        return lax.rem(y + (dy + NY) % NY, NY)

    def plane_dev(dy, dx, dc):
        return ((z * NY + y_at(dy)) * ROW + row_id(dx, dc),)

    def col_dev(dz, dy):
        return ((NY * lax.rem(z + (dz + NZ) % NZ, NZ) + y_at(dy)) * ROW + i,)

    def send(src, dst, ssem, rsem, dev):
        pltpu.make_async_remote_copy(src_ref=src, dst_ref=dst, send_sem=ssem, recv_sem=rsem, device_id=dev,
                                     device_id_type=MESH).start()

    def wait(ref, sem):
        pltpu.make_async_copy(ref, ref, sem).wait()

    def load(src, dst, sem):
        c = pltpu.make_async_copy(src, dst, sem)
        c.start()
        return c

    def load_qkv(l):
        base = i * (heads * hd)
        got = []
        for j in range(heads):
            rows = pl.ds(base + j * hd, hd)
            got.append(load(wk_ref.at[l, rows], wkv_s.at[l, j, 0:hd], lsem.at[l, 2 * j]))
            got.append(load(wv_ref.at[l, rows], wkv_s.at[l, j, hd:wide], lsem.at[l, 2 * j + 1]))
        got.append(load(wq_ref.at[l, pl.ds(base, heads * hd)], wq_s.at[l], lsem.at[l, 2 * heads]))
        return got

    def load_mlp(l):
        return [load(w.at[l], wm.at[l, i, k], msem.at[l, k]) for k, w in enumerate((wg_ref, wu_ref, wd_ref))]

    mlp_loads = [load_mlp(0)]
    qkv_loads = [load_qkv(0)]
    wo_loads = [load(wo_ref.at[0], wo_s.at[0], wosem.at[0])]
    mlp_loads.append(load_mlp(1))
    qkv_loads.append(load_qkv(1))
    wo_loads.append(load(wo_ref.at[1], wo_s.at[1], wosem.at[1]))

    kvbuf[...] = jnp.zeros_like(kvbuf)
    barrier = pltpu.get_barrier_semaphore()
    partners = [plane_dev(*s) for s in PLANE_STEPS] + [col_dev(*s) for s in COL_STEPS if s[0]]
    for dev in partners:
        pl.semaphore_signal(barrier, inc=1, device_id=dev, device_id_type=MESH)
    hrow[pl.ds(i, 1)] = h_ref[...][None]
    lane = lax.broadcasted_iota(jnp.int32, (1, wide), 1)
    pos = f32(r * rtok + lax.broadcasted_iota(jnp.int32, (rtok, 1), 0))
    angles = pos * freq_ref[...]
    cos_tab = jnp.cos(angles)
    sin_tab = jnp.sin(angles)
    sin_tab = jnp.where(lax.rem(lane, hd) < half, -sin_tab, sin_tab)
    phase('barrier')
    pl.semaphore_wait(barrier, len(partners))

    hu = units // 2
    spans = (pl.ds(0, 2), pl.ds(2, 1))
    low, high = pl.ds(0, hu), pl.ds(hu, hu)

    def blk(l, p, dx, dc, rows=None):
        if rows is None:
            return wm.at[l, row_id(dx, dc), spans[p]]
        return wm.at[l, row_id(dx, dc), spans[p], rows]

    def g_push(l, p, k, ref, dx, dc):
        send(ref, ref, gsend.at[l, p, k], grecv.at[l, p, k], row_dev(dx, dc))

    def g_send(l, p):
        for c in (mlp_loads[l][:2], mlp_loads[l][2:])[p]:
            c.wait()
        own = blk(l, p, 0, 0)
        g_push(l, p, 1, own, 1, 0)
        g_push(l, p, 2, own, -1, 0)
        g_push(l, p, 0, own, 0, 1)

    def g_fwd(l, p):
        wait(blk(l, p, -1, 0), grecv.at[l, p, 1])
        g_push(l, p, 3, blk(l, p, -1, 0, low), 1, 0)
        wait(blk(l, p, 1, 0), grecv.at[l, p, 2])
        g_push(l, p, 4, blk(l, p, 1, 0, high), -1, 0)
        g_push(l, p, 5, blk(l, p, -1, 0), 0, 1)
        g_push(l, p, 6, blk(l, p, 1, 0), 0, 1)

    def g_fwd2(l, p):
        for k, rows in enumerate((low, high)):
            wait(blk(l, p, 2, 0, rows), grecv.at[l, p, 3 + k])
            g_push(l, p, 7 + k, blk(l, p, 2, 0, rows), 0, 1)

    def g_done(l, p):
        wait(blk(l, p, 0, 1), grecv.at[l, p, 0])
        wait(blk(l, p, -1, 1), grecv.at[l, p, 5])
        wait(blk(l, p, 1, 1), grecv.at[l, p, 6])
        for k, rows in enumerate((low, high)):
            wait(blk(l, p, 2, 1, rows), grecv.at[l, p, 7 + k])

    def g_drain(l, p):
        for k in (0, 1, 2, 5, 6):
            wait(blk(l, p, 0, 0), gsend.at[l, p, k])
        for k in (3, 4, 7, 8):
            wait(blk(l, p, 0, 0, low), gsend.at[l, p, k])

    length = len_ref[0]

    def turned(p, c, s):
        swapped = jnp.where(lax.rem(lane, hd) < half, pltpu.roll(p, wide - half, 1), pltpu.roll(p, half, 1))
        return p * c + swapped * s

    hidden = f32(h_ref[...])
    for l in range(layers):
        g_attn = f32(gattn_ref[...])[l:l + 1]
        g_mlp = f32(gmlp_ref[...])[l:l + 1]
        phase(f'row_h#l={l}')
        own = h_ref if l == 0 else hloc.at[0]
        for k, s in enumerate(ROW_STEPS):
            send(own, hrow.at[i], asend.at[k], arecv.at[k], row_dev(*s))
        if l == 0:
            g_send(0, 0)
        for k, (dx, dc) in enumerate(ROW_STEPS):
            wait(hrow.at[row_id(-dx, dc)], arecv.at[k])
        phase(f'qkv#l={l}')
        zs[0:rtok] = bf(norm_rows(f32(hrow[...]).reshape(rtok, d_model), g_attn))
        for c in qkv_loads[l]:
            c.wait()
        kv = dot_nt(zs[0:rtok], wkv_s[l].reshape(heads * wide, d_model))
        for j in range(heads):
            p = kv[:, j * wide:(j + 1) * wide]
            kvs[j] = bf(jnp.where(lane < hd, turned(p, cos_tab, sin_tab), p))
        for dz in (3, 2, 1, 0):
            @pl.when(z + dz < NZ)
            def _():
                for dy in (2, 1, 3, 0):
                    if dz or dy:
                        send(kvs.at[y_at(dy)], kvbuf.at[r], kvsend.at[dz, dy], kvrecv.at[dz, dy], col_dev(dz, dy))
        kvbuf[pl.ds(r, 1)] = kvs[pl.ds(y, 1)]
        q = dot_nt(zs[0:rtok], wq_s[l])
        for j in range(0, heads, 2):
            pair = turned(q[:, j * hd:(j + 2) * hd], cos_tab, sin_tab)
            qs[j] = bf(jnp.where(lane < hd, pair, 0.0))
            qs[j + 1] = bf(jnp.where(lane < hd, pltpu.roll(pair, hd, 1), 0.0))
        for dy in (2, 1, 3):
            send(qs.at[y_at(dy)], qbuf.at[y], qsend.at[dy], qrecv.at[dy], col_dev(0, dy))
        qbuf[pl.ds(y, 1)] = qs[pl.ds(y, 1)]
        phase(f'kv_wait#l={l}')
        for dy in (1, 3, 2):
            wait(qbuf.at[y_at(-dy)], qrecv.at[dy])
        for dz in range(NZ):
            @pl.when(z - dz >= 0)
            def _():
                for dy in range(NY):
                    if dz or dy:
                        wait(kvbuf.at[(z - dz) * NY + y_at(-dy)], kvrecv.at[dz, dy])
        phase(f'attn#l={l}')
        keys = COL * rtok
        quer = NY * rtok
        kv_all = kvbuf[...].reshape(keys, wide)
        scores = dot_nt(qbuf[...].reshape(quer, wide), kv_all) * hd ** -0.5
        k_pos = lax.broadcasted_iota(jnp.int32, scores.shape, 1)
        q_pos = z * quer + lax.broadcasted_iota(jnp.int32, scores.shape, 0)
        scores = jnp.where((k_pos <= q_pos) & (k_pos < length), scores, -1e30)
        e = jnp.exp(scores - jnp.max(scores, axis=-1, keepdims=True))
        probs = bf(e * (1.0 / jnp.sum(e, axis=-1, keepdims=True)))
        pv = jnp.dot(probs, kv_all, preferred_element_type=jnp.float32)
        ctx = jnp.where(lax.rem(y, 2) == 0, pltpu.roll(pv, hd, 1), pv)
        cs[...] = bf(ctx.reshape(NY * ROW, tok, wide))
        phase(f'ctx#l={l}')
        slot = ROW * y + i
        for k, (dy, dx, dc) in enumerate(PLANE_STEPS):
            send(cs.at[ROW * y_at(dy) + row_id(dx, dc)], cbuf.at[slot], csend.at[k], crecv.at[k], plane_dev(dy, dx, dc))
        cbuf[pl.ds(slot, 1)] = cs[pl.ds(slot, 1)]
        phase(f'g_b#l={l}')
        if l == 0:
            g_fwd(0, 0)
            g_send(0, 1)
        else:
            g_fwd(1, 1)
            g_fwd2(1, 0)
        wo_loads[l].wait()
        phase(f'ctx_wait#l={l}')
        for k, (dy, dx, dc) in enumerate(PLANE_STEPS):
            wait(cbuf.at[ROW * y_at(-dy) + row_id(-dx, dc)], crecv.at[k])
        phase(f'out#l={l}')
        pieces = []
        for k in range(ROW):
            for j in range(0, heads, 2):
                pieces.append(jnp.where(lane < hd, cbuf[j * ROW + k], cbuf[(j + 1) * ROW + k]))
        ctx_all = jnp.concatenate(pieces, axis=1)
        attn_out = jnp.dot(ctx_all, wo_s[l], preferred_element_type=jnp.float32)
        hid_b = bf(hidden + attn_out)
        hidden = f32(hid_b)
        hloc[1] = hid_b
        hcol[0] = hid_b
        phase(f'col_h#l={l}')
        for k, s in enumerate(COL_STEPS):
            send(hloc.at[1], hcol.at[k + 1], hsend.at[k], hrecv.at[k], col_dev(*s))
        if l == 0:
            g_fwd(0, 1)
            g_fwd2(0, 0)
        else:
            g_fwd2(1, 1)
        phase(f'col_h_wait#l={l}')
        for k in range(COL - 1):
            wait(hcol.at[k + 1], hrecv.at[k])
        zs[...] = bf(norm_rows(f32(hcol[...]).reshape(COL * tok, d_model), g_mlp))
        phase(f'g_done#l={l}')
        g_done(l, 0)
        phase(f'mlp_up#l={l}')
        grp = ROW // 2
        ulane = lax.broadcasted_iota(jnp.int32, (1, grp * units), 1) // units
        for b in range(2):
            gate = dot_nt(zs[...], wm[l, b * grp:(b + 1) * grp, 0].reshape(grp * units, d_model))
            up = dot_nt(zs[...], wm[l, b * grp:(b + 1) * grp, 1].reshape(grp * units, d_model))
            act = bf(gate * (1.0 / (1.0 + jnp.exp(-gate))) * up)
            for j in range(grp):
                acts[b, j * COL * tok:(j + 1) * COL * tok] = jnp.where(ulane == j, act, jnp.zeros_like(act))
        phase(f'g_done2#l={l}')
        if l == 0:
            g_fwd2(0, 1)
            g_send(1, 0)
            g_send(1, 1)
        g_done(l, 1)
        phase(f'mlp_down#l={l}')
        parts = 4
        width = d_model // parts
        for n in range(parts):
            cols = slice(n * width, (n + 1) * width)
            total = jnp.zeros((COL * tok, width), jnp.float32)
            for b in range(2):
                wd = wm[l, b * grp:(b + 1) * grp, 2, :, cols].reshape(grp * units, width)
                prod = jnp.dot(acts[b], wd, preferred_element_type=jnp.float32)
                for j in range(grp):
                    total = total + f32(bf(prod[j * COL * tok:(j + 1) * COL * tok]))
            ysend[:, :, cols] = total.reshape(COL, tok, width)
            for k, (dz, dy) in enumerate(COL_STEPS):
                send(ysend.at[k + 1, :, cols], ybuf.at[k, :, cols], ssend.at[k], srecv.at[k], col_dev(-dz, -dy))
        phase(f'rs_wait#l={l}')
        if l == 0:
            g_fwd(1, 0)
        total = ysend[0]
        for k in range(COL - 1):
            wait(ybuf.at[k], srecv.at[k])
            total = total + ybuf[k]
        hid_b = bf(hidden + total)
        hidden = f32(hid_b)
        phase(f'drain#l={l}')
        for k in range(ROW - 1):
            wait(own, asend.at[k])
        for k in range(len(PLANE_STEPS)):
            wait(cs.at[0], csend.at[k])
        for dz in range(NZ):
            @pl.when(z + dz < NZ)
            def _():
                for dy in range(NY):
                    if dz or dy:
                        wait(kvs.at[0], kvsend.at[dz, dy])
        for dy in (1, 2, 3):
            wait(qs.at[0], qsend.at[dy])
        for k in range(COL - 1):
            wait(hloc.at[1], hsend.at[k])
            wait(ysend.at[0], ssend.at[k])
        if l < layers - 1:
            hloc[0] = hid_b
            hrow[pl.ds(i, 1)] = hid_b[None]
    phase('end')
    for l in range(layers):
        g_drain(l, 0)
        g_drain(l, 1)
    out_ref[...] = bf(norm_rows(hidden, f32(gfin_ref[...])[None]))
    phase()


def solution(mesh):
    def device_fn(hidden_in, lengths, attn_norm, w_query, w_key, w_value, w_out, mlp_norm, w_gate, w_up, w_down, final_norm):
        batch, tok, d_model = hidden_in.shape
        layers, _, heads, head_dim = w_query.shape
        units = w_gate.shape[2]
        half = head_dim // 2
        freq = ROPE_BASE ** (-2.0 * np.arange(half, dtype=np.float32) / head_dim)
        freq = jnp.asarray(np.tile(freq.astype(np.float32), 4)[None])

        def by_rows(w):
            return jnp.transpose(w, (0, 2, 3, 1)).reshape(layers, heads * head_dim, d_model)

        part = heads // ROW
        wide = 2 * head_dim
        dma = pltpu.SemaphoreType.DMA
        b16 = jnp.bfloat16
        vm = pl.BlockSpec(memory_space=pltpu.VMEM)
        hbm = pl.BlockSpec(memory_space=pl.ANY)
        rtok = ROW * tok
        out = pl.pallas_call(
            kernel,
            name='prefill',
            out_shape=jax.ShapeDtypeStruct((tok, d_model), b16),
            in_specs=[vm, pl.BlockSpec(memory_space=pltpu.SMEM), vm, vm, vm, vm] + [hbm] * 7,
            out_specs=vm,
            scratch_shapes=[
                pltpu.VMEM((ROW, tok, d_model), b16),
                pltpu.VMEM((layers, part * head_dim, d_model), b16),
                pltpu.VMEM((layers, part, wide, d_model), b16),
                pltpu.VMEM((layers, heads * head_dim, d_model), b16),
                pltpu.VMEM((layers, ROW, 3, units, d_model), b16),
                pltpu.VMEM((part, rtok, wide), b16),
                pltpu.VMEM((COL, rtok, wide), b16),
                pltpu.VMEM((part, rtok, wide), b16),
                pltpu.VMEM((NY, rtok, wide), b16),
                pltpu.VMEM((NY * ROW, tok, wide), b16),
                pltpu.VMEM((NY * ROW, tok, wide), b16),
                pltpu.VMEM((2, tok, d_model), b16),
                pltpu.VMEM((COL, tok, d_model), b16),
                pltpu.VMEM((COL * tok, d_model), b16),
                pltpu.VMEM((2, ROW // 2 * COL * tok, ROW // 2 * units), b16),
                pltpu.VMEM((COL, tok, d_model), jnp.float32),
                pltpu.VMEM((COL - 1, tok, d_model), jnp.float32),
                dma((layers, 2 * part + 1)), dma((layers,)), dma((layers, 3)),
                dma((ROW - 1,)), dma((ROW - 1,)),
                dma((NZ, NY)), dma((NZ, NY)), dma((NY,)), dma((NY,)),
                dma((NY * ROW - 1,)), dma((NY * ROW - 1,)),
                dma((COL - 1,)), dma((COL - 1,)),
                dma((COL - 1,)), dma((COL - 1,)),
                dma((layers, 2, 9)), dma((layers, 2, 9)),
            ],
            compiler_params=pltpu.CompilerParams(collective_id=0, has_side_effects=True, vmem_limit_bytes=60 * 1024 * 1024),
        )(hidden_in.reshape(tok, d_model), lengths, attn_norm, mlp_norm, final_norm, freq,
          by_rows(w_query), by_rows(w_key), by_rows(w_value), w_out.reshape(layers, heads * head_dim, d_model),
          jnp.transpose(w_gate, (0, 2, 1)), jnp.transpose(w_up, (0, 2, 1)), w_down)
        return out.reshape(batch, tok, d_model)

    seq_part = P(None, 'tp', None)
    in_specs = (seq_part, P(), P(), P(), P(), P(), P(), P(), P(None, None, 'tp'), P(None, None, 'tp'), P(None, 'tp', None), P())
    return jax.shard_map(device_fn, mesh=mesh, in_specs=in_specs, out_specs=seq_part, check_vma=False)
```

time: 121 us -> 115 us (0.950)
  Pallas kernels: 117 us -> 112 us
  local copies, waits for them, and re-layouts: 2.67 us -> 1.38 us
    pallas_call x1, Pallas kernels: 117 us -> 112 us  [device_fn(): pl.pallas_call(kernel, name='prefill', out_shape=jax.ShapeDtypeStruct((to...]
    reshape x1 -> x0, local copies, waits for them, and re-layouts: 1.29 us -> none  [device_fn(): final_norm.reshape(1, d_model)]
where the time goes in v2:
time: 115 us
  Pallas kernels  112 us (97%)
  local copies, waits for them, and re-layouts  1.38 us (1%)
    pallas_call x1, Pallas kernels, device_fn(): pl.pallas_call(kernel, name='prefill', out_shape=jax.ShapeDtypeStruct((to...  112 us

profile of v2, /device:TPU:1, one launch (start us, length us, event | category | flops | bytes accessed | tf_op | source)
XLA Modules:
  0.0 114.5 jit_solution(9022954582077805571)
XLA Ops:
  0.7 112.5 %prefill.1 = bf16[8,2048]{1,0:T(8,128)(2,1)} custom-call(bf16[8,2048]{1,0:T(8,128)(2,1)} %bitcast.21, s32[1]{0:T(128)S(6)} %copy.15.len_ref, bf16[2,2048]{1,0:T(2,128)(2,1)} %gattn_ref.1, bf16[2,2048]{1,0:T(2,128)(2,1)} %gmlp_ref.1, bf16[2048]{0:T(1024)(128)(2,1)} %gfin_ref.1, f32[1,128]{1,0:T(1,128)} %constant.2.clone.freq_ref, ...), custom_call_target="tpu_custom_call" | custom-call | tf_op jit(solution)/shard_map/prefill/pallas_call | solution.py:371
  113.1 1.4 %copy.16 = bf16[1,8,2048]{2,1,0:T(8,128)(2,1)} copy(bf16[1,8,2048]{2,1,0:T(8,128)(2,1)} %bitcast.20) | data formatting | bytes 65536

commit v3 on v2

--- a/solution.py
+++ b/solution.py
@@ -17,7 +17,7 @@
 
 ROW_STEPS = [(2, 1), (2, 0), (1, 1), (3, 1), (1, 0), (3, 0), (0, 1)]
 COL_STEPS = sorted(((dz, dy) for dz in range(NZ) for dy in range(NY) if dz or dy),
-                   key=lambda s: -(min(s[0], 4 - s[0]) + min(s[1], 4 - s[1])))
+                   key=lambda s: min(s[0], 4 - s[0]) + min(s[1], 4 - s[1]))
 PLANE_STEPS = sorted(((dy, dx, dc) for dy in range(NY) for dx in range(NX) for dc in range(2) if dy or dx or dc),
                      key=lambda s: -(min(s[0], 4 - s[0]) + min(s[1], 4 - s[1])))
 
@@ -51,10 +51,10 @@
     return h * inv * gain
 
 
-def kernel(h_ref, len_ref, gattn_ref, gmlp_ref, gfin_ref, freq_ref, wq_ref, wk_ref, wv_ref, wo_ref, wg_ref, wu_ref, wd_ref,
+def kernel(h_in, len_in, gattn_in, gmlp_in, gfin_in, freq_in, wq_ref, wk_ref, wv_ref, wo_ref, wg_ref, wu_ref, wd_ref,
            out_ref,
-           hrow, wq_s, wkv_s, wo_s, wm, kvs, kvbuf, qs, qbuf, cs, cbuf, hloc, hcol, zs, acts, ysend, ybuf,
-           lsem, wosem, msem, asend, arecv, kvsend, kvrecv, qsend, qrecv, csend, crecv, hsend, hrecv, ssend, srecv, gsend, grecv):
+           h_ref, len_ref, gattn_ref, gmlp_ref, gfin_ref, freq_ref, out_s, hrow, wq_s, wkv_s, wo_s, wm, kvs, kvbuf, qs, qbuf, cs, cbuf, hloc, hcol, zs, acts, ysend, ybuf,
+           isem, lsem, wosem, msem, asend, arecv, kvsend, kvrecv, qsend, qrecv, csend, crecv, hsend, hrecv, ssend, srecv, gsend, grecv):
     phase = Phases()
     phase('start')
     layers = wo_s.shape[0]
@@ -112,26 +112,26 @@
     def load_mlp(l):
         return [load(w.at[l], wm.at[l, i, k], msem.at[l, k]) for k, w in enumerate((wg_ref, wu_ref, wd_ref))]
 
+    h_load = load(h_in, h_ref, isem.at[0])
+    barrier = pltpu.get_barrier_semaphore()
+    partners = [plane_dev(*s) for s in PLANE_STEPS] + [col_dev(*s) for s in COL_STEPS if s[0]]
+    for dev in partners:
+        pl.semaphore_signal(barrier, inc=1, device_id=dev, device_id_type=MESH)
+    inputs = [load(src, dst, isem.at[k + 1]) for k, (src, dst) in enumerate((
+        (freq_in, freq_ref), (gattn_in, gattn_ref), (gmlp_in, gmlp_ref), (gfin_in, gfin_ref),
+        (len_in, len_ref)))]
     mlp_loads = [load_mlp(0)]
     qkv_loads = [load_qkv(0)]
     wo_loads = [load(wo_ref.at[0], wo_s.at[0], wosem.at[0])]
     mlp_loads.append(load_mlp(1))
     qkv_loads.append(load_qkv(1))
     wo_loads.append(load(wo_ref.at[1], wo_s.at[1], wosem.at[1]))
-
-    kvbuf[...] = jnp.zeros_like(kvbuf)
-    barrier = pltpu.get_barrier_semaphore()
-    partners = [plane_dev(*s) for s in PLANE_STEPS] + [col_dev(*s) for s in COL_STEPS if s[0]]
-    for dev in partners:
-        pl.semaphore_signal(barrier, inc=1, device_id=dev, device_id_type=MESH)
-    hrow[pl.ds(i, 1)] = h_ref[...][None]
-    lane = lax.broadcasted_iota(jnp.int32, (1, wide), 1)
-    pos = f32(r * rtok + lax.broadcasted_iota(jnp.int32, (rtok, 1), 0))
-    angles = pos * freq_ref[...]
-    cos_tab = jnp.cos(angles)
-    sin_tab = jnp.sin(angles)
-    sin_tab = jnp.where(lax.rem(lane, hd) < half, -sin_tab, sin_tab)
+    for zz in range(1, NZ):
+        @pl.when(zz > z)
+        def _():
+            kvbuf[zz * NY:(zz + 1) * NY] = jnp.zeros((NY, rtok, wide), kvbuf.dtype)
     phase('barrier')
+    h_load.wait()
     pl.semaphore_wait(barrier, len(partners))
 
     hu = units // 2
@@ -180,25 +180,34 @@
         for k in (3, 4, 7, 8):
             wait(blk(l, p, 0, 0, low), gsend.at[l, p, k])
 
-    length = len_ref[0]
 
     def turned(p, c, s):
         swapped = jnp.where(lax.rem(lane, hd) < half, pltpu.roll(p, wide - half, 1), pltpu.roll(p, half, 1))
         return p * c + swapped * s
 
-    hidden = f32(h_ref[...])
     for l in range(layers):
+        phase(f'row_h#l={l}')
+        if l == 0:
+            for k, s in enumerate(ROW_STEPS):
+                send(h_ref, hrow.at[i], asend.at[k], arecv.at[k], row_dev(*s))
+            g_send(0, 0)
+            hrow[pl.ds(i, 1)] = h_ref[...][None]
+            for c in inputs:
+                c.wait()
+            lane = lax.broadcasted_iota(jnp.int32, (1, wide), 1)
+            pos = f32(r * rtok + lax.broadcasted_iota(jnp.int32, (rtok, 1), 0))
+            angles = pos * freq_ref[...]
+            cos_tab = jnp.cos(angles)
+            sin_tab = jnp.sin(angles)
+            sin_tab = jnp.where(lax.rem(lane, hd) < half, -sin_tab, sin_tab)
+        for k, (dx, dc) in enumerate(ROW_STEPS):
+            wait(hrow.at[row_id(-dx, dc)], arecv.at[k])
+        length = len_ref[0]
+        if l == 1:
+            g_fwd(1, 0)
+        phase(f'qkv#l={l}')
         g_attn = f32(gattn_ref[...])[l:l + 1]
         g_mlp = f32(gmlp_ref[...])[l:l + 1]
-        phase(f'row_h#l={l}')
-        own = h_ref if l == 0 else hloc.at[0]
-        for k, s in enumerate(ROW_STEPS):
-            send(own, hrow.at[i], asend.at[k], arecv.at[k], row_dev(*s))
-        if l == 0:
-            g_send(0, 0)
-        for k, (dx, dc) in enumerate(ROW_STEPS):
-            wait(hrow.at[row_id(-dx, dc)], arecv.at[k])
-        phase(f'qkv#l={l}')
         zs[0:rtok] = bf(norm_rows(f32(hrow[...]).reshape(rtok, d_model), g_attn))
         for c in qkv_loads[l]:
             c.wait()
@@ -230,6 +239,8 @@
                 for dy in range(NY):
                     if dz or dy:
                         wait(kvbuf.at[(z - dz) * NY + y_at(-dy)], kvrecv.at[dz, dy])
+        for k in range(ROW - 1):
+            wait(h_ref, asend.at[k])
         phase(f'attn#l={l}')
         keys = COL * rtok
         quer = NY * rtok
@@ -250,11 +261,10 @@
         cbuf[pl.ds(slot, 1)] = cs[pl.ds(slot, 1)]
         phase(f'g_b#l={l}')
         if l == 0:
+            g_send(0, 1)
             g_fwd(0, 0)
-            g_send(0, 1)
         else:
             g_fwd(1, 1)
-            g_fwd2(1, 0)
         wo_loads[l].wait()
         phase(f'ctx_wait#l={l}')
         for k, (dy, dx, dc) in enumerate(PLANE_STEPS):
@@ -265,66 +275,84 @@
             for j in range(0, heads, 2):
                 pieces.append(jnp.where(lane < hd, cbuf[j * ROW + k], cbuf[(j + 1) * ROW + k]))
         ctx_all = jnp.concatenate(pieces, axis=1)
-        attn_out = jnp.dot(ctx_all, wo_s[l], preferred_element_type=jnp.float32)
-        hid_b = bf(hidden + attn_out)
-        hidden = f32(hid_b)
-        hloc[1] = hid_b
-        hcol[0] = hid_b
+        for n in range(2):
+            cols = slice(n * (d_model // 2), (n + 1) * (d_model // 2))
+            attn_out = jnp.dot(ctx_all, wo_s[l, :, cols], preferred_element_type=jnp.float32)
+            hid = bf(f32(h_ref[:, cols] if l == 0 else hloc[2 * l - 1, :, cols]) + attn_out)
+            hloc[2 * l, :, cols] = hid
+            hcol[0, :, cols] = hid
+            for k, s in enumerate(COL_STEPS[:COL // 2 - 1]):
+                send(hloc.at[2 * l, :, cols], hcol.at[k + 1, :, cols], hsend.at[k], hrecv.at[k], col_dev(*s))
+        for k, s in list(enumerate(COL_STEPS))[COL // 2 - 1:]:
+            send(hloc.at[2 * l], hcol.at[k + 1], hsend.at[k], hrecv.at[k], col_dev(*s))
         phase(f'col_h#l={l}')
-        for k, s in enumerate(COL_STEPS):
-            send(hloc.at[1], hcol.at[k + 1], hsend.at[k], hrecv.at[k], col_dev(*s))
         if l == 0:
             g_fwd(0, 1)
-            g_fwd2(0, 0)
-        else:
-            g_fwd2(1, 1)
-        phase(f'col_h_wait#l={l}')
-        for k in range(COL - 1):
-            wait(hcol.at[k + 1], hrecv.at[k])
-        zs[...] = bf(norm_rows(f32(hcol[...]).reshape(COL * tok, d_model), g_mlp))
-        phase(f'g_done#l={l}')
-        g_done(l, 0)
-        phase(f'mlp_up#l={l}')
+        g_fwd2(l, 0)
         grp = ROW // 2
         ulane = lax.broadcasted_iota(jnp.int32, (1, grp * units), 1) // units
-        for b in range(2):
-            gate = dot_nt(zs[...], wm[l, b * grp:(b + 1) * grp, 0].reshape(grp * units, d_model))
-            up = dot_nt(zs[...], wm[l, b * grp:(b + 1) * grp, 1].reshape(grp * units, d_model))
-            act = bf(gate * (1.0 / (1.0 + jnp.exp(-gate))) * up)
-            for j in range(grp):
-                acts[b, j * COL * tok:(j + 1) * COL * tok] = jnp.where(ulane == j, act, jnp.zeros_like(act))
-        phase(f'g_done2#l={l}')
-        if l == 0:
-            g_fwd2(0, 1)
-            g_send(1, 0)
-            g_send(1, 1)
-        g_done(l, 1)
-        phase(f'mlp_down#l={l}')
         parts = 4
         width = d_model // parts
+        halves = 1 if l == 0 else 2
+        slots = COL // halves
+        m = slots * tok
+        for part in range(halves):
+            phase(f'col_h_wait#l={l}#p={part}')
+            for k in range(part * slots, (part + 1) * slots):
+                if k:
+                    wait(hcol.at[k], hrecv.at[k - 1])
+            mine = slice(part * slots, (part + 1) * slots)
+            zs[0:m] = bf(norm_rows(f32(hcol[mine]).reshape(m, d_model), g_mlp))
+            if part == 0:
+                phase(f'g_done#l={l}')
+                g_done(l, 0)
+            phase(f'mlp_up#l={l}#p={part}')
+            for b in range(2):
+                gate = dot_nt(zs[0:m], wm[l, b * grp:(b + 1) * grp, 0].reshape(grp * units, d_model))
+                up = dot_nt(zs[0:m], wm[l, b * grp:(b + 1) * grp, 1].reshape(grp * units, d_model))
+                act = bf(gate * (1.0 / (1.0 + jnp.exp(-gate))) * up)
+                for j in range(grp):
+                    acts[b, j * m:(j + 1) * m] = jnp.where(ulane == j, act, jnp.zeros_like(act))
+                if part == 0 and b == 0:
+                    phase(f'g_fwd2#l={l}')
+                    g_fwd2(l, 1)
+                    phase(f'mlp_up2#l={l}#p={part}')
+            if part == 0:
+                phase(f'g_done2#l={l}')
+                if l == 0:
+                    g_send(1, 0)
+                g_done(l, 1)
+            phase(f'mlp_down#l={l}#p={part}')
+            for n in range(parts):
+                cols = slice(n * width, (n + 1) * width)
+                total = jnp.zeros((m, width), jnp.float32)
+                for b in range(2):
+                    wd = wm[l, b * grp:(b + 1) * grp, 2, :, cols].reshape(grp * units, width)
+                    prod = jnp.dot(acts[b, 0:grp * m], wd, preferred_element_type=jnp.float32)
+                    for j in range(grp):
+                        total = total + f32(bf(prod[j * m:(j + 1) * m]))
+                ysend[mine, :, cols] = total.reshape(slots, tok, width)
+                for k in reversed(range(part * slots, (part + 1) * slots)):
+                    if k:
+                        dz, dy = COL_STEPS[k - 1]
+                        send(ysend.at[k, :, cols], ybuf.at[k - 1, :, cols], ssend.at[k - 1], srecv.at[k - 1, n],
+                             col_dev(-dz, -dy))
+        phase(f'rs_wait#l={l}')
         for n in range(parts):
             cols = slice(n * width, (n + 1) * width)
-            total = jnp.zeros((COL * tok, width), jnp.float32)
-            for b in range(2):
-                wd = wm[l, b * grp:(b + 1) * grp, 2, :, cols].reshape(grp * units, width)
-                prod = jnp.dot(acts[b], wd, preferred_element_type=jnp.float32)
-                for j in range(grp):
-                    total = total + f32(bf(prod[j * COL * tok:(j + 1) * COL * tok]))
-            ysend[:, :, cols] = total.reshape(COL, tok, width)
-            for k, (dz, dy) in enumerate(COL_STEPS):
-                send(ysend.at[k + 1, :, cols], ybuf.at[k, :, cols], ssend.at[k], srecv.at[k], col_dev(-dz, -dy))
-        phase(f'rs_wait#l={l}')
+            total = ysend[0, :, cols]
+            for k in range(COL - 1):
+                wait(ybuf.at[k, :, cols], srecv.at[k, n])
+                total = total + ybuf[k, :, cols]
+            hid = bf(f32(hloc[2 * l, :, cols]) + total)
+            hloc[2 * l + 1, :, cols] = hid
+            if l < layers - 1:
+                hrow[pl.ds(i, 1), :, cols] = hid[None]
+                for k, s in enumerate(ROW_STEPS):
+                    send(hloc.at[2 * l + 1, :, cols], hrow.at[i, :, cols], asend.at[k], arecv.at[k], row_dev(*s))
         if l == 0:
-            g_fwd(1, 0)
-        total = ysend[0]
-        for k in range(COL - 1):
-            wait(ybuf.at[k], srecv.at[k])
-            total = total + ybuf[k]
-        hid_b = bf(hidden + total)
-        hidden = f32(hid_b)
+            g_send(1, 1)
         phase(f'drain#l={l}')
-        for k in range(ROW - 1):
-            wait(own, asend.at[k])
         for k in range(len(PLANE_STEPS)):
             wait(cs.at[0], csend.at[k])
         for dz in range(NZ):
@@ -336,16 +364,15 @@
         for dy in (1, 2, 3):
             wait(qs.at[0], qsend.at[dy])
         for k in range(COL - 1):
-            wait(hloc.at[1], hsend.at[k])
+            wait(hloc.at[2 * l], hsend.at[k])
             wait(ysend.at[0], ssend.at[k])
-        if l < layers - 1:
-            hloc[0] = hid_b
-            hrow[pl.ds(i, 1)] = hid_b[None]
     phase('end')
     for l in range(layers):
         g_drain(l, 0)
         g_drain(l, 1)
-    out_ref[...] = bf(norm_rows(hidden, f32(gfin_ref[...])[None]))
+    out_s[...] = bf(norm_rows(f32(hloc[2 * layers - 1]), f32(gfin_ref[...])[None]))
+    c = load(out_s, out_ref, isem.at[0])
+    c.wait()
     phase()
 
 
@@ -365,16 +392,22 @@
         wide = 2 * head_dim
         dma = pltpu.SemaphoreType.DMA
         b16 = jnp.bfloat16
-        vm = pl.BlockSpec(memory_space=pltpu.VMEM)
         hbm = pl.BlockSpec(memory_space=pl.ANY)
         rtok = ROW * tok
         out = pl.pallas_call(
             kernel,
             name='prefill',
             out_shape=jax.ShapeDtypeStruct((tok, d_model), b16),
-            in_specs=[vm, pl.BlockSpec(memory_space=pltpu.SMEM), vm, vm, vm, vm] + [hbm] * 7,
-            out_specs=vm,
+            in_specs=[hbm, pl.BlockSpec(memory_space=pltpu.HBM)] + [hbm] * 11,
+            out_specs=hbm,
             scratch_shapes=[
+                pltpu.VMEM((tok, d_model), b16),
+                pltpu.SMEM((1,), jnp.int32),
+                pltpu.VMEM((layers, d_model), b16),
+                pltpu.VMEM((layers, d_model), b16),
+                pltpu.VMEM((d_model,), b16),
+                pltpu.VMEM((1, 4 * half), jnp.float32),
+                pltpu.VMEM((tok, d_model), b16),
                 pltpu.VMEM((ROW, tok, d_model), b16),
                 pltpu.VMEM((layers, part * head_dim, d_model), b16),
                 pltpu.VMEM((layers, part, wide, d_model), b16),
@@ -386,18 +419,18 @@
                 pltpu.VMEM((NY, rtok, wide), b16),
                 pltpu.VMEM((NY * ROW, tok, wide), b16),
                 pltpu.VMEM((NY * ROW, tok, wide), b16),
-                pltpu.VMEM((2, tok, d_model), b16),
+                pltpu.VMEM((2 * layers, tok, d_model), b16),
                 pltpu.VMEM((COL, tok, d_model), b16),
                 pltpu.VMEM((COL * tok, d_model), b16),
                 pltpu.VMEM((2, ROW // 2 * COL * tok, ROW // 2 * units), b16),
                 pltpu.VMEM((COL, tok, d_model), jnp.float32),
                 pltpu.VMEM((COL - 1, tok, d_model), jnp.float32),
-                dma((layers, 2 * part + 1)), dma((layers,)), dma((layers, 3)),
+                dma((6,)), dma((layers, 2 * part + 1)), dma((layers,)), dma((layers, 3)),
                 dma((ROW - 1,)), dma((ROW - 1,)),
                 dma((NZ, NY)), dma((NZ, NY)), dma((NY,)), dma((NY,)),
                 dma((NY * ROW - 1,)), dma((NY * ROW - 1,)),
                 dma((COL - 1,)), dma((COL - 1,)),
-                dma((COL - 1,)), dma((COL - 1,)),
+                dma((COL - 1,)), dma((COL - 1, 4)),
                 dma((layers, 2, 9)), dma((layers, 2, 9)),
             ],
             compiler_params=pltpu.CompilerParams(collective_id=0, has_side_effects=True, vmem_limit_bytes=60 * 1024 * 1024),

time: 115 us -> 106 us (0.922)
  Pallas kernels: 112 us -> 103 us
    pallas_call x1, Pallas kernels: 112 us -> 103 us  [device_fn(): pl.pallas_call(kernel, name='prefill', out_shape=jax.ShapeDtypeStruct((to...]
where the time goes in v3:
time: 106 us; the launch traced here: 105 us
  Pallas kernels  103 us (97%)
  local copies, waits for them, and re-layouts  1.38 us (1%)
    pallas_call x1, Pallas kernels, device_fn(): pl.pallas_call(kernel, name='prefill', out_shape=jax.ShapeDtypeStruct((to...  103 us

profile of v3, /device:TPU:1, one launch (start us, length us, event | category | flops | bytes accessed | tf_op | source)
XLA Modules:
  0.0 105.3 jit_solution(11436754979019061987)
XLA Ops:
  0.7 103.3 %prefill.1 = bf16[8,2048]{1,0:T(8,128)(2,1)} custom-call(bf16[8,2048]{1,0:T(8,128)(2,1)} %bitcast.21, s32[1]{0:T(128)S(6)} %copy.15.len_in, bf16[2,2048]{1,0:T(2,128)(2,1)} %gattn_in.1, bf16[2,2048]{1,0:T(2,128)(2,1)} %gmlp_in.1, bf16[2048]{0:T(1024)(128)(2,1)} %gfin_in.1, f32[1,128]{1,0:T(1,128)} %constant.2.clone.freq_in, bf16[2,2048,2048]{2,1,0:T(8,128)(2,1)} %bitcast.14, ...), custom_call_target="tpu_custom_call" | custom-call | tf_op jit(solution)/shard_map/prefill/pallas_call | solution.py:397
  103.9 1.4 %copy.16 = bf16[1,8,2048]{2,1,0:T(8,128)(2,1)} copy(bf16[1,8,2048]{2,1,0:T(8,128)(2,1)} %bitcast.20) | data formatting | bytes 65536

commit v4 on v3

--- a/solution.py
+++ b/solution.py
@@ -16,8 +16,9 @@
 COL = NY * NZ
 
 ROW_STEPS = [(2, 1), (2, 0), (1, 1), (3, 1), (1, 0), (3, 0), (0, 1)]
-COL_STEPS = sorted(((dz, dy) for dz in range(NZ) for dy in range(NY) if dz or dy),
-                   key=lambda s: min(s[0], 4 - s[0]) + min(s[1], 4 - s[1]))
+COL_STEPS = [(0, 2), (1, 0), (3, 0), (2, 0), (1, 2), (3, 2), (2, 2),
+             (0, 1), (0, 3), (1, 1), (1, 3), (3, 1), (3, 3), (2, 1), (2, 3)]
+SLOT = {s: k for k, s in enumerate([(0, 0)] + COL_STEPS)}
 PLANE_STEPS = sorted(((dy, dx, dc) for dy in range(NY) for dx in range(NX) for dc in range(2) if dy or dx or dc),
                      key=lambda s: -(min(s[0], 4 - s[0]) + min(s[1], 4 - s[1])))
 
@@ -53,8 +54,8 @@
 
 def kernel(h_in, len_in, gattn_in, gmlp_in, gfin_in, freq_in, wq_ref, wk_ref, wv_ref, wo_ref, wg_ref, wu_ref, wd_ref,
            out_ref,
-           h_ref, len_ref, gattn_ref, gmlp_ref, gfin_ref, freq_ref, out_s, hrow, wq_s, wkv_s, wo_s, wm, kvs, kvbuf, qs, qbuf, cs, cbuf, hloc, hcol, zs, acts, ysend, ybuf,
-           isem, lsem, wosem, msem, asend, arecv, kvsend, kvrecv, qsend, qrecv, csend, crecv, hsend, hrecv, ssend, srecv, gsend, grecv):
+           h_ref, len_ref, gattn_ref, gmlp_ref, gfin_ref, freq_ref, hrow, wq_s, wkv_s, wo_s, wm, kvs, kvbuf, qs, qbuf, cs, cbuf, hloc, hcol, zs, acts, ysend, y1, yst, y2,
+           isem, lsem, wosem, msem, asend, arecv, kvsend, kvrecv, qsend, qrecv, csend, crecv, hsend, hrecv, s1send, s1recv, s2send, s2recv, gsend, grecv):
     phase = Phases()
     phase('start')
     layers = wo_s.shape[0]
@@ -86,6 +87,12 @@
 
     def col_dev(dz, dy):
         return ((NY * lax.rem(z + (dz + NZ) % NZ, NZ) + y_at(dy)) * ROW + i,)
+
+    def first_slot(n, step, g):
+        return SLOT[(g, step) if n % 2 == 0 else (step, g)]
+
+    def back(n, step):
+        return col_dev(0, -step) if n % 2 == 0 else col_dev(-step, 0)
 
     def send(src, dst, ssem, rsem, dev):
         pltpu.make_async_remote_copy(src_ref=src, dst_ref=dst, send_sem=ssem, recv_sem=rsem, device_id=dev,
@@ -266,19 +273,26 @@
         else:
             g_fwd(1, 1)
         wo_loads[l].wait()
-        phase(f'ctx_wait#l={l}')
-        for k, (dy, dx, dc) in enumerate(PLANE_STEPS):
-            wait(cbuf.at[ROW * y_at(-dy) + row_id(-dx, dc)], crecv.at[k])
-        phase(f'out#l={l}')
-        pieces = []
-        for k in range(ROW):
-            for j in range(0, heads, 2):
-                pieces.append(jnp.where(lane < hd, cbuf[j * ROW + k], cbuf[(j + 1) * ROW + k]))
-        ctx_all = jnp.concatenate(pieces, axis=1)
+        attn_out = jnp.zeros((tok, d_model), jnp.float32)
+        for step in (0, 1, 3, 2):
+            phase(f'ctx_wait#l={l}#s={step}')
+            for k, (dy, dx, dc) in enumerate(PLANE_STEPS):
+                if dx == step:
+                    wait(cbuf.at[ROW * y_at(-dy) + row_id(-dx, dc)], crecv.at[k])
+            phase(f'out#l={l}#s={step}')
+            chip = lax.rem(x - step + NX, NX)
+            pieces = []
+            for c in range(2):
+                for j in range(0, heads, 2):
+                    pieces.append(jnp.where(lane < hd, cbuf[j * ROW + 2 * chip + c], cbuf[(j + 1) * ROW + 2 * chip + c]))
+            ctx_chip = jnp.concatenate(pieces, axis=1)
+            rows = pl.ds(pl.multiple_of(chip * (2 * heads * hd), 2 * heads * hd), 2 * heads * hd)
+            if step != 2:
+                attn_out = attn_out + jnp.dot(ctx_chip, wo_s[l, rows, :], preferred_element_type=jnp.float32)
         for n in range(2):
             cols = slice(n * (d_model // 2), (n + 1) * (d_model // 2))
-            attn_out = jnp.dot(ctx_all, wo_s[l, :, cols], preferred_element_type=jnp.float32)
-            hid = bf(f32(h_ref[:, cols] if l == 0 else hloc[2 * l - 1, :, cols]) + attn_out)
+            part_out = attn_out[:, cols] + jnp.dot(ctx_chip, wo_s[l, rows, cols], preferred_element_type=jnp.float32)
+            hid = bf(f32(h_ref[:, cols] if l == 0 else hloc[2 * l - 1, :, cols]) + part_out)
             hloc[2 * l, :, cols] = hid
             hcol[0, :, cols] = hid
             for k, s in enumerate(COL_STEPS[:COL // 2 - 1]):
@@ -289,6 +303,8 @@
         if l == 0:
             g_fwd(0, 1)
         g_fwd2(l, 0)
+        if l == 1:
+            g_fwd2(1, 1)
         grp = ROW // 2
         ulane = lax.broadcasted_iota(jnp.int32, (1, grp * units), 1) // units
         parts = 4
@@ -313,9 +329,9 @@
                 act = bf(gate * (1.0 / (1.0 + jnp.exp(-gate))) * up)
                 for j in range(grp):
                     acts[b, j * m:(j + 1) * m] = jnp.where(ulane == j, act, jnp.zeros_like(act))
-                if part == 0 and b == 0:
+                if l == 0 and b == 0:
                     phase(f'g_fwd2#l={l}')
-                    g_fwd2(l, 1)
+                    g_fwd2(0, 1)
                     phase(f'mlp_up2#l={l}#p={part}')
             if part == 0:
                 phase(f'g_done2#l={l}')
@@ -332,18 +348,30 @@
                     for j in range(grp):
                         total = total + f32(bf(prod[j * m:(j + 1) * m]))
                 ysend[mine, :, cols] = total.reshape(slots, tok, width)
-                for k in reversed(range(part * slots, (part + 1) * slots)):
-                    if k:
-                        dz, dy = COL_STEPS[k - 1]
-                        send(ysend.at[k, :, cols], ybuf.at[k - 1, :, cols], ssend.at[k - 1], srecv.at[k - 1, n],
-                             col_dev(-dz, -dy))
+                for step in (2, 1, 3):
+                    for g in range(4):
+                        k = first_slot(n, step, g)
+                        if part * slots <= k < (part + 1) * slots:
+                            send(ysend.at[k, :, cols], y1.at[n, step - 1, g], s1send.at[n, step - 1], s1recv.at[n, step - 1],
+                                 back(n, step))
         phase(f'rs_wait#l={l}')
         for n in range(parts):
             cols = slice(n * width, (n + 1) * width)
-            total = ysend[0, :, cols]
-            for k in range(COL - 1):
-                wait(ybuf.at[k, :, cols], srecv.at[k, n])
-                total = total + ybuf[k, :, cols]
+            sums = [ysend[first_slot(n, 0, g), :, cols] for g in range(4)]
+            for step in (1, 3, 2):
+                wait(y1.at[n, step - 1], s1recv.at[n, step - 1])
+                sums = [t + y1[n, step - 1, g] for g, t in enumerate(sums)]
+            for g in range(4):
+                yst[n, g] = sums[g]
+            for g in (2, 1, 3):
+                send(yst.at[n, g], y2.at[n, g - 1], s2send.at[n, g - 1], s2recv.at[n, g - 1], back(n + 1, g))
+        phase(f'rs2_wait#l={l}')
+        for n in range(parts):
+            cols = slice(n * width, (n + 1) * width)
+            total = yst[n, 0]
+            for g in (1, 3, 2):
+                wait(y2.at[n, g - 1], s2recv.at[n, g - 1])
+                total = total + y2[n, g - 1]
             hid = bf(f32(hloc[2 * l, :, cols]) + total)
             hloc[2 * l + 1, :, cols] = hid
             if l < layers - 1:
@@ -363,16 +391,16 @@
                         wait(kvs.at[0], kvsend.at[dz, dy])
         for dy in (1, 2, 3):
             wait(qs.at[0], qsend.at[dy])
+            for n in range(parts):
+                wait(y1.at[n, dy - 1], s1send.at[n, dy - 1])
+                wait(yst.at[n, dy], s2send.at[n, dy - 1])
         for k in range(COL - 1):
             wait(hloc.at[2 * l], hsend.at[k])
-            wait(ysend.at[0], ssend.at[k])
     phase('end')
     for l in range(layers):
         g_drain(l, 0)
         g_drain(l, 1)
-    out_s[...] = bf(norm_rows(f32(hloc[2 * layers - 1]), f32(gfin_ref[...])[None]))
-    c = load(out_s, out_ref, isem.at[0])
-    c.wait()
+    out_ref[...] = bf(norm_rows(f32(hloc[2 * layers - 1]), f32(gfin_ref[...])[None]))
     phase()
 
 
@@ -397,9 +425,9 @@
         out = pl.pallas_call(
             kernel,
             name='prefill',
-            out_shape=jax.ShapeDtypeStruct((tok, d_model), b16),
+            out_shape=pltpu.VMEM((tok, d_model), b16),
             in_specs=[hbm, pl.BlockSpec(memory_space=pltpu.HBM)] + [hbm] * 11,
-            out_specs=hbm,
+            out_specs=pl.BlockSpec(memory_space=pltpu.VMEM),
             scratch_shapes=[
                 pltpu.VMEM((tok, d_model), b16),
                 pltpu.SMEM((1,), jnp.int32),
@@ -407,7 +435,6 @@
                 pltpu.VMEM((layers, d_model), b16),
                 pltpu.VMEM((d_model,), b16),
                 pltpu.VMEM((1, 4 * half), jnp.float32),
-                pltpu.VMEM((tok, d_model), b16),
                 pltpu.VMEM((ROW, tok, d_model), b16),
                 pltpu.VMEM((layers, part * head_dim, d_model), b16),
                 pltpu.VMEM((layers, part, wide, d_model), b16),
@@ -424,13 +451,15 @@
                 pltpu.VMEM((COL * tok, d_model), b16),
                 pltpu.VMEM((2, ROW // 2 * COL * tok, ROW // 2 * units), b16),
                 pltpu.VMEM((COL, tok, d_model), jnp.float32),
-                pltpu.VMEM((COL - 1, tok, d_model), jnp.float32),
+                pltpu.VMEM((4, 3, 4, tok, d_model // 4), jnp.float32),
+                pltpu.VMEM((4, 4, tok, d_model // 4), jnp.float32),
+                pltpu.VMEM((4, 3, tok, d_model // 4), jnp.float32),
                 dma((6,)), dma((layers, 2 * part + 1)), dma((layers,)), dma((layers, 3)),
                 dma((ROW - 1,)), dma((ROW - 1,)),
                 dma((NZ, NY)), dma((NZ, NY)), dma((NY,)), dma((NY,)),
                 dma((NY * ROW - 1,)), dma((NY * ROW - 1,)),
                 dma((COL - 1,)), dma((COL - 1,)),
-                dma((COL - 1,)), dma((COL - 1, 4)),
+                dma((4, 3)), dma((4, 3)), dma((4, 3)), dma((4, 3)),
                 dma((layers, 2, 9)), dma((layers, 2, 9)),
             ],
             compiler_params=pltpu.CompilerParams(collective_id=0, has_side_effects=True, vmem_limit_bytes=60 * 1024 * 1024),

time: 106 us -> 96.7 us (0.912)
  Pallas kernels: 103 us -> 95.2 us
    pallas_call x1, Pallas kernels: 103 us -> 95.2 us  [device_fn(): pl.pallas_call(kernel, name='prefill', out_shape=pltpu.VMEM((tok, d_model...]
where the time goes in v4:
time: 96.7 us; the launch traced here: 96.5 us
  Pallas kernels  95.2 us (98%)
    pallas_call x1, Pallas kernels, device_fn(): pl.pallas_call(kernel, name='prefill', out_shape=pltpu.VMEM((tok, d_model...  95.2 us

profile of v4, /device:TPU:1, one launch (start us, length us, event | category | flops | bytes accessed | tf_op | source)
XLA Modules:
  0.0 96.5 jit_solution(12011662118710222069)
XLA Ops:
  0.7 95.2 %prefill.1 = bf16[8,2048]{1,0:T(8,128)(2,1)S(1)} custom-call(bf16[8,2048]{1,0:T(8,128)(2,1)} %bitcast.21, s32[1]{0:T(128)S(6)} %copy.16.len_in, bf16[2,2048]{1,0:T(2,128)(2,1)} %gattn_in.1, bf16[2,2048]{1,0:T(2,128)(2,1)} %gmlp_in.1, bf16[2048]{0:T(1024)(128)(2,1)} %gfin_in.1, f32[1,128]{1,0:T(1,128)} %constant.2.clone.freq_in, ...), custom_call_target="tpu_custom_call" | custom-call | tf_op jit(solution)/shard_map/prefill/pallas_call | solution.py:425
  95.9 0.6 copy.15

commit v5 on v4

--- a/solution.py
+++ b/solution.py
@@ -196,7 +196,8 @@
         phase(f'row_h#l={l}')
         if l == 0:
             for k, s in enumerate(ROW_STEPS):
-                send(h_ref, hrow.at[i], asend.at[k], arecv.at[k], row_dev(*s))
+                if s[1] == 0 or s[0] == 0:
+                    send(h_ref, hrow.at[i], asend.at[k], arecv.at[k], row_dev(*s))
             g_send(0, 0)
             hrow[pl.ds(i, 1)] = h_ref[...][None]
             for c in inputs:
@@ -207,8 +208,14 @@
             cos_tab = jnp.cos(angles)
             sin_tab = jnp.sin(angles)
             sin_tab = jnp.where(lax.rem(lane, hd) < half, -sin_tab, sin_tab)
+        if True:
+            for dx in (1, 3, 2):
+                wait(hrow.at[row_id(-dx, 0)], arecv.at[ROW_STEPS.index((dx, 0))])
+                k = ROW_STEPS.index((dx, 1))
+                send(hrow.at[row_id(-dx, 0)], hrow.at[row_id(-dx, 0)], asend.at[k], arecv.at[k], row_dev(0, 1))
         for k, (dx, dc) in enumerate(ROW_STEPS):
-            wait(hrow.at[row_id(-dx, dc)], arecv.at[k])
+            if dc:
+                wait(hrow.at[row_id(-dx, dc)], arecv.at[k])
         length = len_ref[0]
         if l == 1:
             g_fwd(1, 0)
@@ -377,7 +384,8 @@
             if l < layers - 1:
                 hrow[pl.ds(i, 1), :, cols] = hid[None]
                 for k, s in enumerate(ROW_STEPS):
-                    send(hloc.at[2 * l + 1, :, cols], hrow.at[i, :, cols], asend.at[k], arecv.at[k], row_dev(*s))
+                    if s[1] == 0 or s[0] == 0:
+                        send(hloc.at[2 * l + 1, :, cols], hrow.at[i, :, cols], asend.at[k], arecv.at[k], row_dev(*s))
         if l == 0:
             g_send(1, 1)
         phase(f'drain#l={l}')

time: 96.7 us -> 94.5 us (0.977)
  Pallas kernels: 95.2 us -> 93.1 us
    pallas_call x1, Pallas kernels: 95.2 us -> 93.1 us  [device_fn(): pl.pallas_call(kernel, name='prefill', out_shape=pltpu.VMEM((tok, d_model...]
where the time goes in v5:
time: 94.5 us; the launch traced here: 94.4 us
  Pallas kernels  93.1 us (99%)
    pallas_call x1, Pallas kernels, device_fn(): pl.pallas_call(kernel, name='prefill', out_shape=pltpu.VMEM((tok, d_model...  93.1 us

profile of v5, /device:TPU:1, one launch (start us, length us, event | category | flops | bytes accessed | tf_op | source)
XLA Modules:
  0.0 94.4 jit_solution(8706452072691976742)
XLA Ops:
  0.7 93.1 %prefill.1 = bf16[8,2048]{1,0:T(8,128)(2,1)S(1)} custom-call(bf16[8,2048]{1,0:T(8,128)(2,1)} %bitcast.21, s32[1]{0:T(128)S(6)} %copy.16.len_in, bf16[2,2048]{1,0:T(2,128)(2,1)} %gattn_in.1, bf16[2,2048]{1,0:T(2,128)(2,1)} %gmlp_in.1, bf16[2048]{0:T(1024)(128)(2,1)} %gfin_in.1, f32[1,128]{1,0:T(1,128)} %constant.2.clone.freq_in, ...), custom_call_target="tpu_custom_call" | custom-call | tf_op jit(solution)/shard_map/prefill/pallas_call | solution.py:433
  93.8 0.6 copy.15

commit v6 on v5

--- a/solution.py
+++ b/solution.py
@@ -54,7 +54,7 @@
 
 def kernel(h_in, len_in, gattn_in, gmlp_in, gfin_in, freq_in, wq_ref, wk_ref, wv_ref, wo_ref, wg_ref, wu_ref, wd_ref,
            out_ref,
-           h_ref, len_ref, gattn_ref, gmlp_ref, gfin_ref, freq_ref, hrow, wq_s, wkv_s, wo_s, wm, kvs, kvbuf, qs, qbuf, cs, cbuf, hloc, hcol, zs, acts, ysend, y1, yst, y2,
+           wkv_t, wq_t, wgu_t, h_ref, len_ref, gattn_ref, gmlp_ref, gfin_ref, freq_ref, hrow, wq_s, wkv_s, wo_s, wm, kvs, kvbuf, qs, qbuf, cs, cbuf, hloc, hcol, zs, acts, ysend, y1, yst, y2,
            isem, lsem, wosem, msem, asend, arecv, kvsend, kvrecv, qsend, qrecv, csend, crecv, hsend, hrecv, s1send, s1recv, s2send, s2recv, gsend, grecv):
     phase = Phases()
     phase('start')
@@ -192,6 +192,19 @@
         swapped = jnp.where(lax.rem(lane, hd) < half, pltpu.roll(p, wide - half, 1), pltpu.roll(p, half, 1))
         return p * c + swapped * s
 
+    def turn_qkv(l):
+        for c in qkv_loads[l]:
+            c.wait()
+        for j in range(heads):
+            wkv_t[:, j * wide:(j + 1) * wide] = wkv_s[l, j].T
+        for j in range(heads // 2):
+            wq_t[:, j * wide:(j + 1) * wide] = wq_s[l, j * wide:(j + 1) * wide].T
+
+    def turn_mlp(l):
+        for j in range(0, ROW, 2):
+            for k in range(2):
+                wgu_t[k, :, j * units:(j + 2) * units] = wm[l, j:j + 2, k].reshape(2 * units, d_model).T
+
     for l in range(layers):
         phase(f'row_h#l={l}')
         if l == 0:
@@ -208,6 +221,9 @@
             cos_tab = jnp.cos(angles)
             sin_tab = jnp.sin(angles)
             sin_tab = jnp.where(lax.rem(lane, hd) < half, -sin_tab, sin_tab)
+            phase('turn#l=0')
+            turn_qkv(0)
+            phase('row_wait#l=0')
         if True:
             for dx in (1, 3, 2):
                 wait(hrow.at[row_id(-dx, 0)], arecv.at[ROW_STEPS.index((dx, 0))])
@@ -217,15 +233,11 @@
             if dc:
                 wait(hrow.at[row_id(-dx, dc)], arecv.at[k])
         length = len_ref[0]
-        if l == 1:
-            g_fwd(1, 0)
         phase(f'qkv#l={l}')
         g_attn = f32(gattn_ref[...])[l:l + 1]
         g_mlp = f32(gmlp_ref[...])[l:l + 1]
         zs[0:rtok] = bf(norm_rows(f32(hrow[...]).reshape(rtok, d_model), g_attn))
-        for c in qkv_loads[l]:
-            c.wait()
-        kv = dot_nt(zs[0:rtok], wkv_s[l].reshape(heads * wide, d_model))
+        kv = jnp.dot(zs[0:rtok], wkv_t[...], preferred_element_type=jnp.float32)
         for j in range(heads):
             p = kv[:, j * wide:(j + 1) * wide]
             kvs[j] = bf(jnp.where(lane < hd, turned(p, cos_tab, sin_tab), p))
@@ -236,7 +248,7 @@
                     if dz or dy:
                         send(kvs.at[y_at(dy)], kvbuf.at[r], kvsend.at[dz, dy], kvrecv.at[dz, dy], col_dev(dz, dy))
         kvbuf[pl.ds(r, 1)] = kvs[pl.ds(y, 1)]
-        q = dot_nt(zs[0:rtok], wq_s[l])
+        q = jnp.dot(zs[0:rtok], wq_t[...], preferred_element_type=jnp.float32)
         for j in range(0, heads, 2):
             pair = turned(q[:, j * hd:(j + 2) * hd], cos_tab, sin_tab)
             qs[j] = bf(jnp.where(lane < hd, pair, 0.0))
@@ -278,6 +290,7 @@
             g_send(0, 1)
             g_fwd(0, 0)
         else:
+            g_fwd(1, 0)
             g_fwd(1, 1)
         wo_loads[l].wait()
         attn_out = jnp.zeros((tok, d_model), jnp.float32)
@@ -311,6 +324,10 @@
             g_fwd(0, 1)
         g_fwd2(l, 0)
         if l == 1:
+            g_done(1, 0)
+            phase('turn_mlp')
+            turn_mlp(1)
+            phase(f'col_h2#l={l}')
             g_fwd2(1, 1)
         grp = ROW // 2
         ulane = lax.broadcasted_iota(jnp.int32, (1, grp * units), 1) // units
@@ -326,13 +343,18 @@
                     wait(hcol.at[k], hrecv.at[k - 1])
             mine = slice(part * slots, (part + 1) * slots)
             zs[0:m] = bf(norm_rows(f32(hcol[mine]).reshape(m, d_model), g_mlp))
-            if part == 0:
+            if l == 0:
                 phase(f'g_done#l={l}')
-                g_done(l, 0)
+                g_done(0, 0)
             phase(f'mlp_up#l={l}#p={part}')
             for b in range(2):
-                gate = dot_nt(zs[0:m], wm[l, b * grp:(b + 1) * grp, 0].reshape(grp * units, d_model))
-                up = dot_nt(zs[0:m], wm[l, b * grp:(b + 1) * grp, 1].reshape(grp * units, d_model))
+                if l == 0:
+                    gate = dot_nt(zs[0:m], wm[l, b * grp:(b + 1) * grp, 0].reshape(grp * units, d_model))
+                    up = dot_nt(zs[0:m], wm[l, b * grp:(b + 1) * grp, 1].reshape(grp * units, d_model))
+                else:
+                    these = slice(b * grp * units, (b + 1) * grp * units)
+                    gate = jnp.dot(zs[0:m], wgu_t[0, :, these], preferred_element_type=jnp.float32)
+                    up = jnp.dot(zs[0:m], wgu_t[1, :, these], preferred_element_type=jnp.float32)
                 act = bf(gate * (1.0 / (1.0 + jnp.exp(-gate))) * up)
                 for j in range(grp):
                     acts[b, j * m:(j + 1) * m] = jnp.where(ulane == j, act, jnp.zeros_like(act))
@@ -361,6 +383,9 @@
                         if part * slots <= k < (part + 1) * slots:
                             send(ysend.at[k, :, cols], y1.at[n, step - 1, g], s1send.at[n, step - 1], s1recv.at[n, step - 1],
                                  back(n, step))
+        if l == 0:
+            phase('turn#l=1')
+            turn_qkv(1)
         phase(f'rs_wait#l={l}')
         for n in range(parts):
             cols = slice(n * width, (n + 1) * width)
@@ -437,6 +462,9 @@
             in_specs=[hbm, pl.BlockSpec(memory_space=pltpu.HBM)] + [hbm] * 11,
             out_specs=pl.BlockSpec(memory_space=pltpu.VMEM),
             scratch_shapes=[
+                pltpu.VMEM((d_model, part * wide), b16),
+                pltpu.VMEM((d_model, part * head_dim), b16),
+                pltpu.VMEM((2, d_model, ROW * units), b16),
                 pltpu.VMEM((tok, d_model), b16),
                 pltpu.SMEM((1,), jnp.int32),
                 pltpu.VMEM((layers, d_model), b16),

time: 94.5 us -> 93.9 us (level)
  no operation moved by 1% of the time
where the time goes in v6:
time: 93.9 us; the launch traced here: 93.7 us
  Pallas kernels  92.5 us (99%)
    pallas_call x1, Pallas kernels, device_fn(): pl.pallas_call(kernel, name='prefill', out_shape=pltpu.VMEM((tok, d_model...  92.5 us

profile of v6, /device:TPU:1, one launch (start us, length us, event | category | flops | bytes accessed | tf_op | source)
XLA Modules:
  0.0 93.7 jit_solution(9493911450461381619)
XLA Ops:
  0.7 92.5 %prefill.1 = bf16[8,2048]{1,0:T(8,128)(2,1)S(1)} custom-call(bf16[8,2048]{1,0:T(8,128)(2,1)} %bitcast.21, s32[1]{0:T(128)S(6)} %copy.16.len_in, bf16[2,2048]{1,0:T(2,128)(2,1)} %gattn_in.1, bf16[2,2048]{1,0:T(2,128)(2,1)} %gmlp_in.1, bf16[2048]{0:T(1024)(128)(2,1)} %gfin_in.1, f32[1,128]{1,0:T(1,128)} %constant.2.clone.freq_in, ...), custom_call_target="tpu_custom_call" | custom-call | tf_op jit(solution)/shard_map/prefill/pallas_call | solution.py:458
  93.1 0.6 copy.15

commit v7 on v6

--- a/solution.py
+++ b/solution.py
@@ -15,12 +15,17 @@
 ROW = 2 * NX
 COL = NY * NZ
 
-ROW_STEPS = [(2, 1), (2, 0), (1, 1), (3, 1), (1, 0), (3, 0), (0, 1)]
-COL_STEPS = [(0, 2), (1, 0), (3, 0), (2, 0), (1, 2), (3, 2), (2, 2),
-             (0, 1), (0, 3), (1, 1), (1, 3), (3, 1), (3, 3), (2, 1), (2, 3)]
+
+def far(d):
+    return min(d, NX - d)
+
+
+ROW_STEPS = sorted(((dx, dc) for dx in range(NX) for dc in range(2) if dx or dc), key=lambda s: (-far(s[0]), -s[1]))
+COL_STEPS = sorted(((dz, dy) for dz in range(NZ) for dy in range(NY) if dz or dy),
+                   key=lambda s: (s[1] % 2, s[0] > 0, s[1] * (1 - s[1] % 2), far(s[0]), s))
 SLOT = {s: k for k, s in enumerate([(0, 0)] + COL_STEPS)}
 PLANE_STEPS = sorted(((dy, dx, dc) for dy in range(NY) for dx in range(NX) for dc in range(2) if dy or dx or dc),
-                     key=lambda s: -(min(s[0], 4 - s[0]) + min(s[1], 4 - s[1])))
+                     key=lambda s: -far(s[0]) - far(s[1]))
 
 
 class Phases:

time: 93.9 us -> 93.9 us (level)
  no operation moved by 1% of the time
where the time goes in v7:
time: 93.9 us; the launch traced here: 93.7 us
  Pallas kernels  92.5 us (99%)
    pallas_call x1, Pallas kernels, device_fn(): pl.pallas_call(kernel, name='prefill', out_shape=pltpu.VMEM((tok, d_model...  92.5 us

profile of v7, /device:TPU:1, one launch (start us, length us, event | category | flops | bytes accessed | tf_op | source)
XLA Modules:
  0.0 93.7 jit_solution(9493911450461381619)
XLA Ops:
  0.7 92.5 %prefill.1 = bf16[8,2048]{1,0:T(8,128)(2,1)S(1)} custom-call(bf16[8,2048]{1,0:T(8,128)(2,1)} %bitcast.21, s32[1]{0:T(128)S(6)} %copy.16.len_in, bf16[2,2048]{1,0:T(2,128)(2,1)} %gattn_in.1, bf16[2,2048]{1,0:T(2,128)(2,1)} %gmlp_in.1, bf16[2048]{0:T(1024)(128)(2,1)} %gfin_in.1, f32[1,128]{1,0:T(1,128)} %constant.2.clone.freq_in, ...), custom_call_target="tpu_custom_call" | custom-call | tf_op jit(solution)/shard_map/prefill/pallas_call | solution.py:463
  93.1 0.6 copy.15

commit v8 on v7

--- a/solution.py
+++ b/solution.py
@@ -277,9 +277,9 @@
         quer = NY * rtok
         kv_all = kvbuf[...].reshape(keys, wide)
         scores = dot_nt(qbuf[...].reshape(quer, wide), kv_all) * hd ** -0.5
-        k_pos = lax.broadcasted_iota(jnp.int32, scores.shape, 1)
-        q_pos = z * quer + lax.broadcasted_iota(jnp.int32, scores.shape, 0)
-        scores = jnp.where((k_pos <= q_pos) & (k_pos < length), scores, -1e30)
+        k_pos = lax.broadcasted_iota(jnp.int32, (1, keys), 1)
+        limit = jnp.minimum(z * quer + 1 + lax.broadcasted_iota(jnp.int32, (quer, 1), 0), length)
+        scores = jnp.where(k_pos < limit, scores, -1e30)
         e = jnp.exp(scores - jnp.max(scores, axis=-1, keepdims=True))
         probs = bf(e * (1.0 / jnp.sum(e, axis=-1, keepdims=True)))
         pv = jnp.dot(probs, kv_all, preferred_element_type=jnp.float32)
@@ -392,6 +392,18 @@
             phase('turn#l=1')
             turn_qkv(1)
         phase(f'rs_wait#l={l}')
+        for k in range(len(PLANE_STEPS)):
+            wait(cs.at[0], csend.at[k])
+        for dz in range(NZ):
+            @pl.when(z + dz < NZ)
+            def _():
+                for dy in range(NY):
+                    if dz or dy:
+                        wait(kvs.at[0], kvsend.at[dz, dy])
+        for dy in (1, 2, 3):
+            wait(qs.at[0], qsend.at[dy])
+        for k in range(COL - 1):
+            wait(hloc.at[2 * l], hsend.at[k])
         for n in range(parts):
             cols = slice(n * width, (n + 1) * width)
             sums = [ysend[first_slot(n, 0, g), :, cols] for g in range(4)]
@@ -419,21 +431,10 @@
         if l == 0:
             g_send(1, 1)
         phase(f'drain#l={l}')
-        for k in range(len(PLANE_STEPS)):
-            wait(cs.at[0], csend.at[k])
-        for dz in range(NZ):
-            @pl.when(z + dz < NZ)
-            def _():
-                for dy in range(NY):
-                    if dz or dy:
-                        wait(kvs.at[0], kvsend.at[dz, dy])
-        for dy in (1, 2, 3):
-            wait(qs.at[0], qsend.at[dy])
+        for g in range(3):
             for n in range(parts):
-                wait(y1.at[n, dy - 1], s1send.at[n, dy - 1])
-                wait(yst.at[n, dy], s2send.at[n, dy - 1])
-        for k in range(COL - 1):
-            wait(hloc.at[2 * l], hsend.at[k])
+                wait(y1.at[n, g], s1send.at[n, g])
+                wait(yst.at[n, g + 1], s2send.at[n, g])
     phase('end')
     for l in range(layers):
         g_drain(l, 0)

time: 93.9 us -> 93.5 us (level)
  no operation moved by 1% of the time
where the time goes in v8:
time: 93.5 us; the launch traced here: 93.3 us
  Pallas kernels  92 us (98%)
    pallas_call x1, Pallas kernels, device_fn(): pl.pallas_call(kernel, name='prefill', out_shape=pltpu.VMEM((tok, d_model...  92 us

profile of v8, /device:TPU:1, one launch (start us, length us, event | category | flops | bytes accessed | tf_op | source)
XLA Modules:
  0.0 93.3 jit_solution(6017645522147153683)
XLA Ops:
  0.7 92.0 %prefill.1 = bf16[8,2048]{1,0:T(8,128)(2,1)S(1)} custom-call(bf16[8,2048]{1,0:T(8,128)(2,1)} %bitcast.21, s32[1]{0:T(128)S(6)} %copy.16.len_in, bf16[2,2048]{1,0:T(2,128)(2,1)} %gattn_in.1, bf16[2,2048]{1,0:T(2,128)(2,1)} %gmlp_in.1, bf16[2048]{0:T(1024)(128)(2,1)} %gfin_in.1, f32[1,128]{1,0:T(1,128)} %constant.2.clone.freq_in, ...), custom_call_target="tpu_custom_call" | custom-call | tf_op jit(solution)/shard_map/prefill/pallas_call | solution.py:464
  92.7 0.6 copy.15
